TPU v7x, 32 devices: a whole 2x2x4 slice. The times are simulated.
32 devices in a mesh: row: 8 (over z, y), col: 4 (over x, core).
Axes of the slice: x: 2, y: 2, z: 4, core: 2. Of those that a mesh axis runs over, the one named last changes fastest.
Arguments:
- matrix_tiles: float32 [8, 4, 16, 256, 256], P('row', 'col'), may hold values from -0.3125 to 0.3125
- tile_slot: int32 [8, 4, 16], P('row', 'col'), may hold values from 0 to 2047, as said below
- cost_vector: float32 [512, 256], P('col'), may hold values from -24 to 24
- lower_bound: float32 [512, 256], P('col'), may hold values from -4 to 4
- bound_width: float32 [512, 256], P('col'), may hold values from 0.5 to 4
- variable_kind: int32 [512, 256], P('col'), may hold values from 0 to 2
- right_side: float32 [128, 256], P('row'), may hold values from -24 to 24
- row_kind: int32 [128, 256], P('row'), may hold values from 0 to 1
- primal_start: float32 [512, 256], P('col'), may hold values from -6 to 6
- dual_start: float32 [128, 256], P('row'), may hold values from -3 to 3
- primal_weight: float32 [], replicated, may hold values from 0.7 to 1.4
- step_start: float32 [], replicated, may hold values from 1 to 2
Outputs:
- primal: float32 [512, 256], P('col')
- dual: float32 [128, 256], P('row')
Inputs may be any that keep to these rules, and one draw needn't show every extreme that they name: `tile_slot`: within each block [r, c] the 16 tiles lie in different column tiles. Split a block's 128 column tiles into runs of 16 in a row: no run holds more than 2 of the block's tiles.
All inputs are finite; a program needn't handle non-finite values.
Results may differ from a plain program's by a relative error of at most 0.00026.
Values sent between devices are 32-bit elements; how exact they have to be, the bound alone decides.
No kernel may reach another device: no remote copies, remote signals or barrier semaphores. Data moves between devices by JAX's collectives and lax.ppermute only.
A program may use at most 64 MiB of HBM per device.

v0:
```python
import jax
import jax.numpy as jnp
from jax import lax
from jax.sharding import PartitionSpec as P

ITERS = 4


highest = lax.Precision.HIGHEST


def project_primal(values, lower_bound, bound_width, variable_kind):
    lifted = jnp.where(variable_kind >= 1, jnp.maximum(values, lower_bound), values)
    return jnp.where(variable_kind == 2, jnp.minimum(lifted, lower_bound + bound_width), lifted)


def project_dual(values, row_kind):
    return jnp.where(row_kind == 1, jnp.maximum(values, 0.0), values)


def next_step(cross, dual_square, primal_square, weight, step_size, iteration):
    movement = 0.5 * weight * primal_square + 0.5 * dual_square / weight
    count = iteration + 11.0
    return movement / jnp.maximum(
        jnp.abs(cross) / (1.0 - count ** (-0.3)), movement / ((1.0 + count ** (-0.6)) * step_size)
    )


def shards(
    matrix_tiles,
    tile_slot,
    cost_vector,
    lower_bound,
    bound_width,
    variable_kind,
    right_side,
    row_kind,
    primal_start,
    dual_start,
    primal_weight,
    step_start,
):
    tile_set = matrix_tiles[0, 0]
    slots = tile_slot[0, 0]
    row_tiles, tile_width = right_side.shape
    col_tiles = cost_vector.shape[0]
    tile_count = slots.shape[0]
    row_count = lax.axis_size("row")
    row_of = slots // col_tiles
    col_of = slots % col_tiles
    row_onehot = (row_of[None, :] == jnp.arange(row_tiles, dtype=jnp.int32)[:, None]).astype(
        jnp.float32
    )

    def forward_picked(picked):
        product = jnp.einsum("tij,tj->ti", tile_set, picked, precision=highest)
        partial_rows = jnp.dot(row_onehot, product, precision=highest)
        return lax.psum(partial_rows, "col")

    def backward_product(vector):
        picked = vector[row_of]
        return jnp.einsum("tij,ti->tj", tile_set, picked, precision=highest)

    share_len = col_tiles * tile_width // row_count
    offset = lax.axis_index("row") * share_len

    def take_share(values):
        return lax.dynamic_slice_in_dim(values.reshape(-1), offset, share_len, 0)

    share_tiles = col_tiles // row_count
    capacity = (tile_count + row_count - 1) // row_count
    share_of = col_of // share_tiles
    counter = jnp.arange(tile_count, dtype=jnp.int32)
    earlier = (counter[None, :] < counter[:, None]) & (share_of[None, :] == share_of[:, None])
    position = jnp.sum(earlier.astype(jnp.int32), axis=1)
    destination = share_of * capacity + position
    send_hit = destination[None, :] == jnp.arange(row_count * capacity, dtype=jnp.int32)[:, None]
    send_onehot = send_hit.astype(jnp.float32)
    local_index = col_of % share_tiles
    occupied = jnp.sum(send_hit.astype(jnp.int32), axis=1)
    send_index = jnp.where(
        occupied > 0, jnp.sum(jnp.where(send_hit, local_index[None, :], 0), axis=1), -1
    )
    recv_index = lax.all_to_all(send_index, "row", split_axis=0, concat_axis=0, tiled=True)
    recv_onehot = (recv_index[None, :] == jnp.arange(share_tiles, dtype=jnp.int32)[:, None]).astype(
        jnp.float32
    )
    cost_share = take_share(cost_vector)
    lower_share = take_share(lower_bound)
    width_share = take_share(bound_width)
    kind_share = take_share(variable_kind)

    def reduce_back(vector):
        sent = jnp.dot(send_onehot, backward_product(vector), precision=highest)
        arrived = lax.all_to_all(sent, "row", split_axis=0, concat_axis=0, tiled=True)
        return jnp.dot(recv_onehot, arrived, precision=highest).reshape(-1)

    primal = take_share(primal_start)
    image = forward_picked(primal_start[col_of])
    dual = dual_start
    step_size = step_start
    gradient = reduce_back(dual)
    for iteration in range(ITERS):
        primal_next = project_primal(
            primal - step_size / primal_weight * (cost_share - gradient),
            lower_share,
            width_share,
            kind_share,
        )
        back = jnp.dot(
            recv_onehot.T, primal_next.reshape(share_tiles, tile_width), precision=highest
        )
        returned = lax.all_to_all(back, "row", split_axis=0, concat_axis=0, tiled=True)
        image_next = forward_picked(jnp.dot(send_onehot.T, returned, precision=highest))
        dual_next = project_dual(
            dual + step_size * primal_weight * (right_side - 2.0 * image_next + image), row_kind
        )
        if iteration + 1 < ITERS:
            gradient = reduce_back(dual_next)
            change_dual = dual_next - dual
            change_primal = primal_next - primal
            cross_part = jnp.sum(change_dual * (image_next - image))
            dual_part = jnp.sum(change_dual * change_dual)
            primal_part = jnp.sum(change_primal * change_primal)
            cross, dual_square, primal_rows = lax.psum((cross_part, dual_part, primal_part), "row")
            primal_square = lax.psum(primal_rows, "col")
            step_size = next_step(
                cross, dual_square, primal_square, primal_weight, step_size, iteration
            )
        primal, dual, image = (primal_next, dual_next, image_next)
    primal = lax.all_gather(primal, "row", axis=0, tiled=True).reshape(col_tiles, tile_width)
    return (primal, dual)


def solution(mesh):
    return jax.shard_map(
        shards,
        mesh=mesh,
        in_specs=(
            P("row", "col", None, None, None),
            P("row", "col", None),
            P("col", None),
            P("col", None),
            P("col", None),
            P("col", None),
            P("row", None),
            P("row", None),
            P("col", None),
            P("row", None),
            P(),
            P(),
        ),
        out_specs=(P("col", None), P("row", None)),
        check_vma=False,
    )
```

profile of v0, /device:TPU:0, one launch (start us, length us, event | category | flops | bytes accessed | tf_op | source)
XLA Modules:
  0.0 292.4 jit_solution(2359915443829012869)
XLA Ops:
  0.6 0.7 and_select_fusion.1
  1.7 0.7 select_n.161
  2.4 7.3 %all-to-all-start = ((s32[8,2,1]{1,2,0:T(1,128)}), s32[8,2,1]{1,2,0:T(1,128)S(1)}, u32[]{:S(2)}, u32[]{:S(2)}) async-start(s32[8,2,1]{1,2,0:T(1,128)} %bitcast.1), calls=%async_computation | async-start | bytes 8192 | tf_op jit(solution)/shard_map/all_to_all | solution.py:84
  9.7 0.7 fusion.86
  10.3 1.3 gather_fusion
  11.7 4.3 %fusion.16 = f32[16,1,256]{2,1,0:T(1,128)S(1)} fusion(f32[1,1,16,256,256]{4,3,2,1,0:T(8,128)} %param.12, f32[16,256,1]{1,0,2:T(8,128)S(1)} %bitcast.156), kind=kOutput, calls=%fused_computation.21 | convolution fusion | flops 12582912 | bytes 4227072 | tf_op jit(solution)/shard_map/tij,ti->tj/dot_general | solution.py:62
  16.2 0.6 all_to_all.63
  16.8 0.6 gather_fusion.1
  17.4 6.0 %all-to-all-start.1 = ((f32[8,2,256]{2,1,0:T(2,128)}), f32[8,2,256]{2,1,0:T(2,128)S(1)}, u32[]{:S(2)}, u32[]{:S(2)}) async-start(f32[8,2,256]{2,1,0:T(2,128)} %all_to_all.63), calls=%async_computation.1 | async-start | bytes 32768 | tf_op jit(solution)/shard_map/all_to_all | solution.py:95
  23.4 5.7 %fusion.12 = f32[16,1,256]{2,1,0:T(1,128)S(1)} fusion(f32[1,1,16,256,256]{4,3,2,1,0:T(8,128)} %param.12, f32[16,256,1]{1,0,2:T(8,128)S(1)} %bitcast.154), kind=kOutput, calls=%fused_computation.17 | convolution fusion | flops 12582912 | bytes 4227072 | tf_op jit(solution)/shard_map/tij,tj->ti/dot_general | solution.py:56
  30.9 0.5 broadcast.428
  31.4 0.7 reduce.3
  32.4 0.6 multiply_reduce_fusion.8
  33.0 0.2 fusion.62
  33.2 0.6 copy.28
  33.8 6.0 %all-to-all-start.2 = ((f32[8,2,256]{2,1,0:T(2,128)}), f32[8,2,256]{2,1,0:T(2,128)S(1)}, u32[]{:S(2)}, u32[]{:S(2)}) async-start(f32[8,2,256]{2,1,0:T(2,128)} %copy.28), calls=%async_computation.2 | async-start | bytes 32768 | tf_op jit(solution)/shard_map/all_to_all | solution.py:113
  40.0 6.5 %all-to-all-done.2 = f32[8,2,256]{2,1,0:T(2,128)S(1)} async-done(((f32[8,2,256]{2,1,0:T(2,128)}), f32[8,2,256]{2,1,0:T(2,128)S(1)}, u32[]{:S(2)}, u32[]{:S(2)}) %all-to-all-start.2) | async-done | bytes 16416 | tf_op jit(solution)/shard_map/all_to_all | solution.py:113
  46.4 0.2 convolution_bitcast_fusion.6
  46.6 5.7 %fusion.14 = f32[16,1,256]{2,1,0:T(1,128)S(1)} fusion(f32[1,1,16,256,256]{4,3,2,1,0:T(8,128)} %param.12, f32[16,256,1]{1,0,2:T(8,128)S(1)} %convolution_bitcast_fusion.6), kind=kOutput, calls=%fused_computation.19 | convolution fusion | flops 12582912 | bytes 4227072 | tf_op jit(solution)/shard_map/tij,tj->ti/dot_general | solution.py:56
  52.4 10.5 %all-reduce.3 = (f32[16,256]{1,0:T(8,128)S(1)}, f32[16,256]{1,0:T(8,128)S(1)}) all-reduce(f32[16,256]{1,0:T(8,128)S(1)} %fusion.30, f32[16,256]{1,0:T(8,128)S(1)} %fusion.32), channel_id=1, replica_groups=mesh['row'=8,'col'=4] {'col'}, use_global_device_ids=true, to_apply=%region_7.8 | all-reduce | flops 8192 | bytes 65536 | tf_op jit(solution)/shard_map/psum | solution.py:58
  62.9 0.7 multiply_reduce_fusion.6
  63.6 0.6 gather_fusion.2
  64.2 4.3 %fusion.10 = f32[16,1,256]{2,1,0:T(1,128)S(1)} fusion(f32[1,1,16,256,256]{4,3,2,1,0:T(8,128)} %param.12, f32[16,256,1]{1,0,2:T(8,128)S(1)} %bitcast.157), kind=kOutput, calls=%fused_computation.15 | convolution fusion | flops 12582912 | bytes 4227072 | tf_op jit(solution)/shard_map/tij,ti->tj/dot_general | solution.py:62
  68.6 0.6 all_to_all.69
  69.3 3.3 %all-to-all-start.3 = ((f32[8,2,256]{2,1,0:T(2,128)}), f32[8,2,256]{2,1,0:T(2,128)S(1)}, u32[]{:S(2)}, u32[]{:S(2)}) async-start(f32[8,2,256]{2,1,0:T(2,128)} %all_to_all.69), calls=%async_computation.3 | async-start | bytes 32768 | tf_op jit(solution)/shard_map/all_to_all | solution.py:95
  72.6 22.5 %all-reduce.2 = (f32[]{:T(128)}, f32[]{:T(128)}, f32[]{:T(128)}) all-reduce(f32[]{:T(128)} %get-tuple-element.29, f32[]{:T(128)} %get-tuple-element.7, f32[]{:T(128)} %get-tuple-element.6), channel_id=1, replica_groups=mesh['row'=8,'col'=4] {'row'}, use_global_device_ids=true, to_apply=%region_4.5 | all-reduce | flops 3 | bytes 24 | tf_op jit(solution)/shard_map/psum | solution.py:125
  95.1 6.3 %psum.120 = f32[]{:T(128)} all-reduce(f32[]{:T(128)} %get-tuple-element.16), channel_id=1, replica_groups=mesh['row'=8,'col'=4] {'col'}, use_global_device_ids=true, to_apply=%region_5.6 | all-reduce | flops 1 | bytes 8 | tf_op jit(solution)/shard_map/psum | solution.py:126
  103.6 0.6 multiply_reduce_fusion.5
  104.2 0.2 fusion.60
  104.4 0.6 copy.29
  105.0 3.3 %all-to-all-start.4 = ((f32[8,2,256]{2,1,0:T(2,128)}), f32[8,2,256]{2,1,0:T(2,128)S(1)}, u32[]{:S(2)}, u32[]{:S(2)}) async-start(f32[8,2,256]{2,1,0:T(2,128)} %copy.29), calls=%async_computation.4 | async-start | bytes 32768 | tf_op jit(solution)/shard_map/all_to_all | solution.py:113
  108.4 6.5 %all-to-all-done.4 = f32[8,2,256]{2,1,0:T(2,128)S(1)} async-done(((f32[8,2,256]{2,1,0:T(2,128)}), f32[8,2,256]{2,1,0:T(2,128)S(1)}, u32[]{:S(2)}, u32[]{:S(2)}) %all-to-all-start.4) | async-done | bytes 16416 | tf_op jit(solution)/shard_map/all_to_all | solution.py:113
  114.9 0.2 convolution_bitcast_fusion.4
  115.1 5.7 %fusion.8 = f32[16,1,256]{2,1,0:T(1,128)S(1)} fusion(f32[1,1,16,256,256]{4,3,2,1,0:T(8,128)} %param.12, f32[16,256,1]{1,0,2:T(8,128)S(1)} %convolution_bitcast_fusion.4), kind=kOutput, calls=%fused_computation.13 | convolution fusion | flops 12582912 | bytes 4227072 | tf_op jit(solution)/shard_map/tij,tj->ti/dot_general | solution.py:56
  120.9 10.1 %psum.127 = f32[16,256]{1,0:T(8,128)S(1)} all-reduce(f32[16,256]{1,0:T(8,128)S(1)} %fusion.26), channel_id=1, replica_groups=mesh['row'=8,'col'=4] {'col'}, use_global_device_ids=true, to_apply=%region_15.16 | all-reduce | flops 4096 | bytes 32768 | tf_op jit(solution)/shard_map/psum | solution.py:58
  131.0 0.7 multiply_reduce_fusion.3
  131.7 0.6 gather_fusion.3
  132.3 4.3 %fusion.6 = f32[16,1,256]{2,1,0:T(1,128)S(1)} fusion(f32[1,1,16,256,256]{4,3,2,1,0:T(8,128)} %param.12, f32[16,256,1]{1,0,2:T(8,128)S(1)} %bitcast.158), kind=kOutput, calls=%fused_computation.11 | convolution fusion | flops 12582912 | bytes 4227072 | tf_op jit(solution)/shard_map/tij,ti->tj/dot_general | solution.py:62
  136.7 0.6 all_to_all.74
  137.3 3.3 %all-to-all-start.5 = ((f32[8,2,256]{2,1,0:T(2,128)}), f32[8,2,256]{2,1,0:T(2,128)S(1)}, u32[]{:S(2)}, u32[]{:S(2)}) async-start(f32[8,2,256]{2,1,0:T(2,128)} %all_to_all.74), calls=%async_computation.5 | async-start | bytes 32768 | tf_op jit(solution)/shard_map/all_to_all | solution.py:95
  140.7 22.5 %all-reduce.1 = (f32[]{:T(128)}, f32[]{:T(128)}, f32[]{:T(128)}) all-reduce(f32[]{:T(128)} %get-tuple-element.25, f32[]{:T(128)} %get-tuple-element.5, f32[]{:T(128)} %get-tuple-element.4), channel_id=1, replica_groups=mesh['row'=8,'col'=4] {'row'}, use_global_device_ids=true, to_apply=%region_13.14 | all-reduce | flops 3 | bytes 24 | tf_op jit(solution)/shard_map/psum | solution.py:125
  163.1 6.3 %psum.126 = f32[]{:T(128)} all-reduce(f32[]{:T(128)} %get-tuple-element.13), channel_id=1, replica_groups=mesh['row'=8,'col'=4] {'col'}, use_global_device_ids=true, to_apply=%region_14.15 | all-reduce | flops 1 | bytes 8 | tf_op jit(solution)/shard_map/psum | solution.py:126
  171.6 0.6 multiply_reduce_fusion.2
  172.4 0.6 copy.30
  173.1 3.6 %all-to-all-start.6 = ((f32[8,2,256]{2,1,0:T(2,128)}), f32[8,2,256]{2,1,0:T(2,128)S(1)}, u32[]{:S(2)}, u32[]{:S(2)}) async-start(f32[8,2,256]{2,1,0:T(2,128)} %copy.30), calls=%async_computation.6 | async-start | bytes 32768 | tf_op jit(solution)/shard_map/all_to_all | solution.py:113
  176.7 6.3 %all-to-all-done.6 = f32[8,2,256]{2,1,0:T(2,128)S(1)} async-done(((f32[8,2,256]{2,1,0:T(2,128)}), f32[8,2,256]{2,1,0:T(2,128)S(1)}, u32[]{:S(2)}, u32[]{:S(2)}) %all-to-all-start.6) | async-done | bytes 16416 | tf_op jit(solution)/shard_map/all_to_all | solution.py:113
  182.9 0.2 convolution_bitcast_fusion.2
  183.1 5.7 %fusion.4 = f32[16,1,256]{2,1,0:T(1,128)S(1)} fusion(f32[1,1,16,256,256]{4,3,2,1,0:T(8,128)} %param.12, f32[16,256,1]{1,0,2:T(8,128)S(1)} %convolution_bitcast_fusion.2), kind=kOutput, calls=%fused_computation.9 | convolution fusion | flops 12582912 | bytes 4227072 | tf_op jit(solution)/shard_map/tij,tj->ti/dot_general | solution.py:56
  188.9 10.1 %psum.132 = f32[16,256]{1,0:T(8,128)S(1)} all-reduce(f32[16,256]{1,0:T(8,128)S(1)} %fusion.22), channel_id=1, replica_groups=mesh['row'=8,'col'=4] {'col'}, use_global_device_ids=true, to_apply=%region_23.24 | all-reduce | flops 4096 | bytes 32768 | tf_op jit(solution)/shard_map/psum | solution.py:58
  199.1 0.7 multiply_reduce_fusion
  199.7 0.6 gather_fusion.4
  200.3 4.3 %fusion.2 = f32[16,1,256]{2,1,0:T(1,128)S(1)} fusion(f32[1,1,16,256,256]{4,3,2,1,0:T(8,128)} %param.12, f32[16,256,1]{1,0,2:T(8,128)S(1)} %bitcast.155), kind=kOutput, calls=%fused_computation.7 | convolution fusion | flops 12582912 | bytes 4227072 | tf_op jit(solution)/shard_map/tij,ti->tj/dot_general | solution.py:62
  204.7 0.6 all_to_all.79
  205.4 3.3 %all-to-all-start.7 = ((f32[8,2,256]{2,1,0:T(2,128)}), f32[8,2,256]{2,1,0:T(2,128)S(1)}, u32[]{:S(2)}, u32[]{:S(2)}) async-start(f32[8,2,256]{2,1,0:T(2,128)} %all_to_all.79), calls=%async_computation.7 | async-start | bytes 32768 | tf_op jit(solution)/shard_map/all_to_all | solution.py:95
  208.7 22.5 %all-reduce = (f32[]{:T(128)}, f32[]{:T(128)}, f32[]{:T(128)}) all-reduce(f32[]{:T(128)} %get-tuple-element.22, f32[]{:T(128)} %get-tuple-element.3, f32[]{:T(128)} %get-tuple-element.2), channel_id=1, replica_groups=mesh['row'=8,'col'=4] {'row'}, use_global_device_ids=true, to_apply=%region_21.22 | all-reduce | flops 3 | bytes 24 | tf_op jit(solution)/shard_map/psum | solution.py:125
  231.2 6.3 %psum.131 = f32[]{:T(128)} all-reduce(f32[]{:T(128)} %get-tuple-element.10), channel_id=1, replica_groups=mesh['row'=8,'col'=4] {'col'}, use_global_device_ids=true, to_apply=%region_22.23 | all-reduce | flops 1 | bytes 8 | tf_op jit(solution)/shard_map/psum | solution.py:126
  239.9 0.6 copy.31
  240.6 3.3 %all-to-all-start.8 = ((f32[8,2,256]{2,1,0:T(2,128)}), f32[8,2,256]{2,1,0:T(2,128)S(1)}, u32[]{:S(2)}, u32[]{:S(2)}) async-start(f32[8,2,256]{2,1,0:T(2,128)} %copy.31), calls=%async_computation.8 | async-start | bytes 32768 | tf_op jit(solution)/shard_map/all_to_all | solution.py:113
  243.9 31.0 %all_gather.3 = f32[32768]{0:T(1024)S(1)} all-gather(f32[4096]{0:T(1024)S(1)} %minimum_select_fusion), channel_id=1, replica_groups=mesh['row'=8,'col'=4] {'row'}, dimensions={0}, use_global_device_ids=true | all-gather | bytes 147456 | tf_op jit(solution)/shard_map/all_gather | solution.py:131
  274.9 0.7 reshape.368
  275.6 0.2 convolution_bitcast_fusion
  275.8 5.7 %fusion = f32[16,1,256]{2,1,0:T(1,128)S(1)} fusion(f32[1,1,16,256,256]{4,3,2,1,0:T(8,128)} %param.12, f32[16,256,1]{1,0,2:T(8,128)S(1)} %convolution_bitcast_fusion), kind=kOutput, calls=%fused_computation.5 | convolution fusion | flops 12582912 | bytes 4227072 | tf_op jit(solution)/shard_map/tij,tj->ti/dot_general | solution.py:56
  281.6 10.1 %psum.135 = f32[16,256]{1,0:T(8,128)S(1)} all-reduce(f32[16,256]{1,0:T(8,128)S(1)} %fusion.18), channel_id=1, replica_groups=mesh['row'=8,'col'=4] {'col'}, use_global_device_ids=true, to_apply=%region_28.29 | all-reduce | flops 4096 | bytes 32768 | tf_op jit(solution)/shard_map/psum | solution.py:58
  291.7 0.6 maximum_select_fusion
  (68 shorter events, 3.2 us)
Async XLA Ops:
  0.6 16.2 %copy-start.1 = (f32[128,256]{1,0:T(8,128)S(1)}, f32[128,256]{1,0:T(8,128)}, u32[]{:S(2)}) copy-start(f32[128,256]{1,0:T(8,128)} %param.20) | copy-start | bytes 393220
  2.4 15.0 %all-to-all-start = ((s32[8,2,1]{1,2,0:T(1,128)}), s32[8,2,1]{1,2,0:T(1,128)S(1)}, u32[]{:S(2)}, u32[]{:S(2)}) async-start(s32[8,2,1]{1,2,0:T(1,128)} %bitcast.1), calls=%async_computation | async-start | bytes 8192 | tf_op jit(solution)/shard_map/all_to_all | solution.py:84
  11.6 18.8 %copy-start.3 = (f32[128,256]{1,0:T(8,128)S(1)}, f32[128,256]{1,0:T(8,128)}, u32[]{:S(2)}) copy-start(f32[128,256]{1,0:T(8,128)} %param.14) | copy-start | bytes 393220
  11.7 18.9 %copy-start.4 = (f32[128,256]{1,0:T(8,128)S(1)}, f32[128,256]{1,0:T(8,128)}, u32[]{:S(2)}) copy-start(f32[128,256]{1,0:T(8,128)} %param.15) | copy-start | bytes 393220
  11.7 18.9 %copy-start.5 = (f32[128,256]{1,0:T(8,128)S(1)}, f32[128,256]{1,0:T(8,128)}, u32[]{:S(2)}) copy-start(f32[128,256]{1,0:T(8,128)} %param.16) | copy-start | bytes 393220
  11.7 19.0 %copy-start.6 = (s32[128,256]{1,0:T(8,128)S(1)}, s32[128,256]{1,0:T(8,128)}, u32[]{:S(2)}) copy-start(s32[128,256]{1,0:T(8,128)} %param.17) | copy-start | bytes 393220
  17.4 14.8 %all-to-all-start.1 = ((f32[8,2,256]{2,1,0:T(2,128)}), f32[8,2,256]{2,1,0:T(2,128)S(1)}, u32[]{:S(2)}, u32[]{:S(2)}) async-start(f32[8,2,256]{2,1,0:T(2,128)} %all_to_all.63), calls=%async_computation.1 | async-start | bytes 32768 | tf_op jit(solution)/shard_map/all_to_all | solution.py:95
  23.4 39.5 %copy-start = (f32[16,256]{1,0:T(8,128)S(1)}, f32[16,256]{1,0:T(8,128)}, u32[]{:S(2)}) copy-start(f32[16,256]{1,0:T(8,128)} %param.21) | copy-start | bytes 49156
  23.4 39.5 %copy-start.2 = (f32[16,256]{1,0:T(8,128)S(1)}, f32[16,256]{1,0:T(8,128)}, u32[]{:S(2)}) copy-start(f32[16,256]{1,0:T(8,128)} %param.18) | copy-start | bytes 49156
  23.4 39.5 %copy-start.7 = (s32[16,256]{1,0:T(8,128)S(1)}, s32[16,256]{1,0:T(8,128)}, u32[]{:S(2)}) copy-start(s32[16,256]{1,0:T(8,128)} %param.19) | copy-start | bytes 49156
  33.8 12.6 %all-to-all-start.2 = ((f32[8,2,256]{2,1,0:T(2,128)}), f32[8,2,256]{2,1,0:T(2,128)S(1)}, u32[]{:S(2)}, u32[]{:S(2)}) async-start(f32[8,2,256]{2,1,0:T(2,128)} %copy.28), calls=%async_computation.2 | async-start | bytes 32768 | tf_op jit(solution)/shard_map/all_to_all | solution.py:113
  69.3 34.1 %all-to-all-start.3 = ((f32[8,2,256]{2,1,0:T(2,128)}), f32[8,2,256]{2,1,0:T(2,128)S(1)}, u32[]{:S(2)}, u32[]{:S(2)}) async-start(f32[8,2,256]{2,1,0:T(2,128)} %all_to_all.69), calls=%async_computation.3 | async-start | bytes 32768 | tf_op jit(solution)/shard_map/all_to_all | solution.py:95
  105.0 9.9 %all-to-all-start.4 = ((f32[8,2,256]{2,1,0:T(2,128)}), f32[8,2,256]{2,1,0:T(2,128)S(1)}, u32[]{:S(2)}, u32[]{:S(2)}) async-start(f32[8,2,256]{2,1,0:T(2,128)} %copy.29), calls=%async_computation.4 | async-start | bytes 32768 | tf_op jit(solution)/shard_map/all_to_all | solution.py:113
  137.3 34.1 %all-to-all-start.5 = ((f32[8,2,256]{2,1,0:T(2,128)}), f32[8,2,256]{2,1,0:T(2,128)S(1)}, u32[]{:S(2)}, u32[]{:S(2)}) async-start(f32[8,2,256]{2,1,0:T(2,128)} %all_to_all.74), calls=%async_computation.5 | async-start | bytes 32768 | tf_op jit(solution)/shard_map/all_to_all | solution.py:95
  173.1 9.9 %all-to-all-start.6 = ((f32[8,2,256]{2,1,0:T(2,128)}), f32[8,2,256]{2,1,0:T(2,128)S(1)}, u32[]{:S(2)}, u32[]{:S(2)}) async-start(f32[8,2,256]{2,1,0:T(2,128)} %copy.30), calls=%async_computation.6 | async-start | bytes 32768 | tf_op jit(solution)/shard_map/all_to_all | solution.py:113
  205.4 34.2 %all-to-all-start.7 = ((f32[8,2,256]{2,1,0:T(2,128)}), f32[8,2,256]{2,1,0:T(2,128)S(1)}, u32[]{:S(2)}, u32[]{:S(2)}) async-start(f32[8,2,256]{2,1,0:T(2,128)} %all_to_all.79), calls=%async_computation.7 | async-start | bytes 32768 | tf_op jit(solution)/shard_map/all_to_all | solution.py:95
  240.6 35.0 %all-to-all-start.8 = ((f32[8,2,256]{2,1,0:T(2,128)}), f32[8,2,256]{2,1,0:T(2,128)S(1)}, u32[]{:S(2)}, u32[]{:S(2)}) async-start(f32[8,2,256]{2,1,0:T(2,128)} %copy.31), calls=%async_computation.8 | async-start | bytes 32768 | tf_op jit(solution)/shard_map/all_to_all | solution.py:113
where the time goes:
time: 294 us; the launch traced here: 292 us
  blocking collectives  158 us (54%)
  matrix products  48.7 us (17%)
  starting transfers between devices  39.6 us (13%)
  waiting for transfers between devices  19.2 us (7%)
  local copies, waits for them, and re-layouts  11.3 us (4%)
  between operations  8.64 us (3%)
  other arithmetic  6.96 us (2%)
    psum x3, blocking collectives, shards(): lax.psum((cross_part, dual_part, primal_part), 'row')  67.4 us
    psum x4, blocking collectives, forward_picked(): return lax.psum(partial_rows, 'col')  40.9 us
    all_gather x1, blocking collectives, shards(): lax.all_gather(primal, 'row', axis=0, tiled=True)  31 us
    dot_general x5, matrix products, forward_picked(): product = jnp.einsum('tij,tj->ti', tile_set, picked, precision=highest)  28.3 us
    all_to_all x4, waiting for transfers between devices, shards(): lax.all_to_all(back, 'row', split_axis=0, concat_axis=0, tiled=True)  19.2 us
    psum x3, blocking collectives, shards(): primal_square = lax.psum(primal_rows, 'col')  18.8 us
    dot_general x4, matrix products, backward_product(): return jnp.einsum('tij,ti->tj', tile_set, picked, precision=highest)  17.2 us
    all_to_all x4, starting transfers between devices, shards(): lax.all_to_all(back, 'row', split_axis=0, concat_axis=0, tiled=True)  16.2 us
  transfers between devices with their start and end apart: 9, of which 3 were waited for; matrix products, arithmetic and copies ran while one was open for 5% of the time, Pallas kernels for 0%

commit v1 on v0

v1 whole, which is shorter than its diff:
```python
import functools

import jax
import jax.numpy as jnp
from jax import lax
from jax.experimental import pallas as pl
from jax.experimental.pallas import tpu as pltpu
from jax.sharding import PartitionSpec as P

ITERS = 4

highest = lax.Precision.HIGHEST


def square_sum(values):
    return jnp.sum(jnp.sum(values, axis=0, keepdims=True), axis=1, keepdims=True)


def columns_of(rows):
    count, width = rows.shape
    padded = jnp.concatenate([rows, jnp.zeros((128 - count, width), rows.dtype)], axis=0)
    return padded.T


def forward(tiles_ref, slots_ref, vector_ref, row_tiles, col_tiles):
    tile_count, height, width = tiles_ref.shape
    lane = lax.broadcasted_iota(jnp.int32, (height, 128), 1)

    def step(t, total):
        slot = slots_ref[t]
        picked = vector_ref[pl.ds(slot % col_tiles, 1), :]
        product = jnp.sum(tiles_ref[t] * picked, axis=1, keepdims=True)
        return total + jnp.where(lane == slot // col_tiles, product, 0.0)

    total = lax.fori_loop(0, tile_count, step, jnp.zeros((height, 128), jnp.float32), unroll=2)
    return total.T[:row_tiles]


def backward(tiles_ref, slots_ref, rows, out_ref, col_tiles):
    tile_count, height, width = tiles_ref.shape
    columns = columns_of(rows)
    lane = lax.broadcasted_iota(jnp.int32, columns.shape, 1)

    def step(t, carry):
        slot = slots_ref[t]
        mine = jnp.where(lane == slot // col_tiles, columns, 0.0)
        picked = jnp.sum(mine, axis=1, keepdims=True)
        out_ref[pl.ds(t, 1), :width] = jnp.sum(tiles_ref[t] * picked, axis=0, keepdims=True)
        return carry

    lax.fori_loop(0, tile_count, step, 0, unroll=2)


def start_kernel(slots_ref, tiles_ref, dual_ref, out_ref, *, col_tiles):
    tile_count, height, width = tiles_ref.shape
    lane = lax.broadcasted_iota(jnp.int32, (1, out_ref.shape[1] - width), 1)
    for t in range(tile_count):
        column = slots_ref[t] % col_tiles
        out_ref[t : t + 1, width:] = jnp.full(lane.shape, column, jnp.int32).astype(jnp.float32)
    backward(tiles_ref, slots_ref, dual_ref[...], out_ref, col_tiles)


def image_kernel(slots_ref, tiles_ref, vector_ref, out_ref):
    out_ref[...] = forward(
        tiles_ref, slots_ref, vector_ref, out_ref.shape[0], vector_ref.shape[0]
    )


def primal_kernel(*refs, iteration, part_count):
    refs = list(refs)
    slots_ref, place_ref, scalars_ref = refs[:3]
    part_refs = refs[3 : 3 + part_count]
    refs = refs[3 + part_count :]
    tiles_ref, primal_ref, cost_ref, lower_ref, width_ref, kind_ref = refs[:6]
    refs = refs[6:]
    if iteration > 0:
        hot_ref, step_ref, moved_ref = refs[:3]
        refs = refs[3:]
    out_ref, primal_out, step_out = refs[:3]
    refs = refs[3:]
    if iteration == 0:
        hot_ref = refs[0]
        refs = refs[1:]
    gather_ref = refs[0]

    width = primal_ref.shape[1]
    col_tiles = primal_ref.shape[0]
    row_tiles = out_ref.shape[0]
    part_rows = part_refs[0].shape[0]
    for k in range(part_count):
        gather_ref[pl.ds(pl.multiple_of(place_ref[k] * part_rows, 8), part_rows), :] = part_refs[k][...]
    weight = scalars_ref[0]
    if iteration == 0:
        number = lax.broadcasted_iota(jnp.int32, hot_ref.shape, 1).astype(jnp.float32)
        hot_ref[...] = (gather_ref[:, width:] == number).astype(jnp.float32)
        step_size = jnp.full((1, 1), scalars_ref[1], jnp.float32)
    else:
        tile_count = tiles_ref.shape[0]
        sources = gather_ref.shape[0] // tile_count
        sums = gather_ref[:tile_count, width:]
        for r in range(1, sources):
            sums = sums + gather_ref[r * tile_count : (r + 1) * tile_count, width:]
        cross = sums[0:1, 0:1]
        dual_square = sums[1:2, 0:1]
        primal_square = moved_ref[0:1, 0:1]
        before = step_ref[0:1, 0:1]
        movement = 0.5 * weight * primal_square + 0.5 * dual_square / weight
        count = iteration - 1 + 11.0
        step_size = movement / jnp.maximum(
            jnp.abs(cross) / (1.0 - count ** (-0.3)),
            movement / ((1.0 + count ** (-0.6)) * before),
        )
    step_out[...] = jnp.broadcast_to(step_size, step_out.shape)
    gradient = lax.dot_general(
        hot_ref[...],
        gather_ref[:, :width],
        (((0,), (0,)), ((), ())),
        precision=highest,
        preferred_element_type=jnp.float32,
    )
    primal = primal_ref[...]
    kind = kind_ref[...]
    lower = lower_ref[...]
    values = primal - (step_size / weight) * (cost_ref[...] - gradient)
    lifted = jnp.where(kind >= 1, jnp.maximum(values, lower), values)
    primal_next = jnp.where(kind == 2, jnp.minimum(lifted, lower + width_ref[...]), lifted)
    primal_out[...] = primal_next
    change = primal_next - primal
    out_ref[:, width:] = jnp.broadcast_to(
        square_sum(change * change), (row_tiles, out_ref.shape[1] - width)
    )
    out_ref[:, :width] = forward(tiles_ref, slots_ref, primal_out, row_tiles, col_tiles)


def dual_kernel(*refs, last, first, part_count, col_tiles):
    refs = list(refs)
    slots_ref, scalars_ref = refs[:2]
    part_refs = refs[2 : 2 + part_count]
    refs = refs[2 + part_count :]
    if first:
        start_refs = refs[:part_count]
        refs = refs[part_count:]
    else:
        image_ref = refs[0]
        refs = refs[1:]
    tiles_ref, step_ref, dual_ref, side_ref, kind_ref, dual_out = refs[:6]
    refs = refs[6:]

    def combined(those):
        values = [ref[...] for ref in those]
        while len(values) > 1:
            values = [values[i] + values[i + 1] for i in range(0, len(values), 2)]
        return values[0]

    width = dual_ref.shape[1]
    weight = scalars_ref[0]
    total = combined(part_refs)
    image_next = total[:, :width]
    image = combined(start_refs) if first else image_ref[...]
    dual = dual_ref[...]
    step_size = step_ref[0:1, 0:1]
    values = dual + (step_size * weight) * (side_ref[...] - 2.0 * image_next + image)
    dual_next = jnp.where(kind_ref[...] == 1, jnp.maximum(values, 0.0), values)
    dual_out[...] = dual_next
    if last:
        return
    out_ref, image_out, moved_out = refs[:3]
    image_out[...] = image_next
    moved_out[...] = total[:8, width : width + 128]
    change = dual_next - dual
    cross = square_sum(change * (image_next - image))
    dual_square = square_sum(change * change)
    extra = (out_ref.shape[0], out_ref.shape[1] - width)
    which = lax.broadcasted_iota(jnp.int32, extra, 0)
    out_ref[:, width:] = jnp.where(
        which == 0, cross, jnp.where(which == 1, dual_square, 0.0)
    )
    backward(tiles_ref, slots_ref, dual_next, out_ref, col_tiles)


def call(kernel, outs, inputs, scratch=(), spaces=None):
    spaces = spaces or {}
    specs = [
        pl.BlockSpec(memory_space=spaces.get(i, pltpu.VMEM)) for i in range(len(inputs))
    ]
    return pl.pallas_call(
        kernel,
        out_shape=outs,
        in_specs=specs,
        out_specs=[pl.BlockSpec(memory_space=pltpu.VMEM) for _ in outs],
        scratch_shapes=scratch,
        compiler_params=pltpu.CompilerParams(vmem_limit_bytes=32 * 1024 * 1024),
    )(*inputs)


def exchange(values, axis, size):
    others = [
        lax.ppermute(values, axis, [(i, i ^ k) for i in range(size)]) for k in range(1, size)
    ]
    return [values] + others


def gather_rows(values, size):
    copies = jnp.broadcast_to(values[None], (size,) + values.shape)
    arrived = lax.all_to_all(copies, "row", split_axis=0, concat_axis=0)
    return [arrived.reshape(-1, values.shape[-1])], jnp.zeros((1,), jnp.int32)


def shards(
    matrix_tiles,
    tile_slot,
    cost_vector,
    lower_bound,
    bound_width,
    variable_kind,
    right_side,
    row_kind,
    primal_start,
    dual_start,
    primal_weight,
    step_start,
):
    tile_set = matrix_tiles[0, 0]
    slots = tile_slot[0, 0]
    row_tiles, width = right_side.shape
    col_tiles = cost_vector.shape[0]
    tile_count = slots.shape[0]
    row_count = lax.axis_size("row")
    col_count = lax.axis_size("col")
    scalars = jnp.stack([primal_weight, step_start])
    f32 = jnp.float32
    smem = pltpu.SMEM
    sent_shape = (tile_count, width + col_tiles)
    image_shape = (row_tiles, width + 128)

    tiles = tile_set
    (sent,) = call(
        functools.partial(start_kernel, col_tiles=col_tiles),
        [jax.ShapeDtypeStruct(sent_shape, f32)],
        [slots, tiles, dual_start],
        spaces={0: smem},
    )
    (image_start,) = call(
        image_kernel,
        [jax.ShapeDtypeStruct((row_tiles, width), f32)],
        [slots, tiles, primal_start],
        spaces={0: smem},
    )
    start_parts = exchange(image_start, "col", col_count)
    primal, dual = primal_start, dual_start
    hot = step_size = moved = image = None
    for iteration in range(ITERS):
        parts, places = gather_rows(sent, row_count)
        first, last = iteration == 0, iteration + 1 == ITERS
        sources = row_count * tile_count
        outs = [
            jax.ShapeDtypeStruct(image_shape, f32),
            jax.ShapeDtypeStruct(primal.shape, f32),
            jax.ShapeDtypeStruct((8, 128), f32),
        ]
        inputs = [slots, places, scalars, *parts, tiles, primal]
        inputs += [cost_vector, lower_bound, bound_width, variable_kind]
        if first:
            outs.append(jax.ShapeDtypeStruct((sources, col_tiles), f32))
        else:
            inputs += [hot, step_size, moved]
        results = call(
            functools.partial(primal_kernel, iteration=iteration, part_count=len(parts)),
            outs,
            inputs,
            scratch=[pltpu.VMEM((sources, width + col_tiles), f32)],
            spaces={0: smem, 1: smem, 2: smem},
        )
        image_part, primal, step_size = results[:3]
        if first:
            hot = results[3]
        parts = exchange(image_part, "col", col_count)
        outs = [jax.ShapeDtypeStruct(dual.shape, f32)]
        if not last:
            outs += [
                jax.ShapeDtypeStruct(sent_shape, f32),
                jax.ShapeDtypeStruct(dual.shape, f32),
                jax.ShapeDtypeStruct((8, 128), f32),
            ]
        inputs = [slots, scalars, *parts]
        inputs += start_parts if first else [image]
        inputs += [tiles, step_size, dual, right_side, row_kind]
        results = call(
            functools.partial(
                dual_kernel, last=last, first=first, part_count=len(parts), col_tiles=col_tiles
            ),
            outs,
            inputs,
            spaces={0: smem, 1: smem},
        )
        dual = results[0]
        if not last:
            sent, image, moved = results[1:]
    return (primal, dual)


def solution(mesh):
    return jax.shard_map(
        shards,
        mesh=mesh,
        in_specs=(
            P("row", "col", None, None, None),
            P("row", "col", None),
            P("col", None),
            P("col", None),
            P("col", None),
            P("col", None),
            P("row", None),
            P("row", None),
            P("col", None),
            P("row", None),
            P(),
            P(),
        ),
        out_specs=(P("col", None), P("row", None)),
        check_vma=False,
    )
```

time: 294 us -> 93.9 us (0.32)
  blocking collectives: 158 us -> 34.7 us
  matrix products: 48.7 us -> 0 us
  starting transfers between devices: 39.6 us -> 17.1 us
  Pallas kernels: 0 us -> 20.4 us
  waiting for transfers between devices: 19.2 us -> 10.4 us
  other arithmetic: 6.96 us -> 0.08 us
  between operations: 8.64 us -> 2.12 us
    psum x10 -> x0, blocking collectives: 127 us -> none  [the longest x3 67.4 us: shards(): lax.psum((cross_part, dual_part, primal_part), 'row')]
    dot_general x30 -> x0, matrix products: 48.7 us -> none  [the longest x5 28.3 us: forward_picked(): product = jnp.einsum('tij,tj->ti', tile_set, picked, precision=highest)]
    all_to_all x0 -> x3, blocking collectives: none -> 34.7 us  [gather_rows(): arrived = lax.all_to_all(copies, 'row', split_axis=0, concat_axis=0)]
    all_to_all x9 -> x1, starting transfers between devices: 39.6 us -> 7.31 us  [gather_rows(): arrived = lax.all_to_all(copies, 'row', split_axis=0, concat_axis=0)]
    all_gather x1 -> x0, blocking collectives: 31 us -> none  [shards(): lax.all_gather(primal, 'row', axis=0, tiled=True)]
    pallas_call x0 -> x10, Pallas kernels: none -> 20.4 us  [call(): pl.pallas_call(kernel, out_shape=outs, in_specs=specs, out_specs=[pl.Bloc...]
    all_to_all x9 -> x1, waiting for transfers between devices: 19.2 us -> 1.87 us  [gather_rows(): arrived = lax.all_to_all(copies, 'row', split_axis=0, concat_axis=0)]
    ppermute x0 -> x15, starting transfers between devices: none -> 9.74 us  [exchange(): lax.ppermute(values, axis, [(i, i ^ k) for i in range(size)])]
  transfers between devices with their start and end apart: 9 -> 16, of which waited for: 3 -> 8; matrix products, arithmetic and copies ran while one was open for 5% -> 0% of each run, Pallas kernels for 0% -> 4%
where the time goes in v1:
time: 93.9 us; the launch traced here: 93.4 us
  blocking collectives  34.7 us (37%)
  Pallas kernels  20.4 us (22%)
  starting transfers between devices  17.1 us (18%)
  waiting for transfers between devices  10.4 us (11%)
  local copies, waits for them, and re-layouts  8.69 us (9%)
  between operations  2.12 us (2%)
    all_to_all x3, blocking collectives, gather_rows(): arrived = lax.all_to_all(copies, 'row', split_axis=0, concat_axis=0)  34.7 us
    pallas_call x10, Pallas kernels, call(): pl.pallas_call(kernel, out_shape=outs, in_specs=specs, out_specs=[pl.Bloc...  20.4 us
    ppermute x15, starting transfers between devices, exchange(): lax.ppermute(values, axis, [(i, i ^ k) for i in range(size)])  9.74 us
    ppermute x15, waiting for transfers between devices, exchange(): lax.ppermute(values, axis, [(i, i ^ k) for i in range(size)])  8.5 us
    unnamed x28, local copies, waits for them, and re-layouts  7.96 us
    all_to_all x1, starting transfers between devices, gather_rows(): arrived = lax.all_to_all(copies, 'row', split_axis=0, concat_axis=0)  7.31 us
  transfers between devices with their start and end apart: 16, of which 8 were waited for; matrix products, arithmetic and copies ran while one was open for 0% of the time, Pallas kernels for 4%

profile of v1, /device:TPU:0, one launch (start us, length us, event | category | flops | bytes accessed | tf_op | source)
XLA Modules:
  0.0 93.4 jit_solution(3284414945915753032)
XLA Ops:
  0.6 0.0 copy-start.13
  0.6 0.0 copy-start
  0.7 2.2 %copy-done = f32[1,1,16,256,256]{4,3,2,1,0:T(8,128)S(1)} copy-done((f32[1,1,16,256,256]{4,3,2,1,0:T(8,128)S(1)}, f32[1,1,16,256,256]{4,3,2,1,0:T(8,128)}, u32[]{:S(2)}) %copy-start) | copy-done | bytes 4194328
  2.8 0.7 copy-done.10
  3.6 0.7 copy-done.12
  4.2 0.0 copy-start.6
  4.2 1.9 %shard_map.131 = f32[16,384]{1,0:T(8,128)S(1)} custom-call(s32[16]{0:T(128)S(1)} %bitcast.24, f32[16,256,256]{2,1,0:T(8,128)S(1)} %bitcast.10, f32[16,256]{1,0:T(8,128)S(1)} %copy-done.10), custom_call_target="tpu_custom_call" | custom-call | tf_op jit(solution)/shard_map/pallas_call | solution.py:186
  6.2 0.7 broadcast_in_dim.8
  6.9 7.3 %all-to-all-start = ((f32[8,16,384]{2,1,0:T(8,128)}), f32[8,16,384]{2,1,0:T(8,128)S(1)}, u32[]{:S(2)}, u32[]{:S(2)}) async-start(f32[8,16,384]{2,1,0:T(8,128)} %broadcast_in_dim.8), calls=%async_computation | async-start | bytes 393216 | tf_op jit(solution)/shard_map/all_to_all | solution.py:205
  14.2 0.0 copy-done.13
  14.2 0.0 copy-done.7
  14.2 0.0 copy-start.1
  14.2 2.2 %copy-done.1 = f32[1,1,16,256,256]{4,3,2,1,0:T(8,128)S(1)} copy-done((f32[1,1,16,256,256]{4,3,2,1,0:T(8,128)S(1)}, f32[1,1,16,256,256]{4,3,2,1,0:T(8,128)}, u32[]{:S(2)}) %copy-start.1) | copy-done | bytes 4194328
  16.4 1.8 %shard_map.133.refs_6_ = f32[16,256]{1,0:T(8,128)S(1)} custom-call(s32[16]{0:T(128)S(1)} %bitcast.25, f32[16,256,256]{2,1,0:T(8,128)S(1)} %bitcast.11, f32[128,256]{1,0:T(8,128)S(1)} %copy-done.7), custom_call_target="tpu_custom_call" | custom-call | tf_op jit(solution)/shard_map/pallas_call | solution.py:186
  18.2 0.7 collective-permute-start.5
  20.2 0.1 pad_maximum_fusion.refs_2_.refs_1_
  20.3 1.9 %all-to-all-done = f32[8,16,384]{2,1,0:T(8,128)S(1)} async-done(((f32[8,16,384]{2,1,0:T(8,128)}), f32[8,16,384]{2,1,0:T(8,128)S(1)}, u32[]{:S(2)}, u32[]{:S(2)}) %all-to-all-start) | async-done | bytes 196640 | tf_op jit(solution)/shard_map/all_to_all | solution.py:205
  22.1 0.0 copy-done.3
  22.1 0.0 copy-done.4
  22.1 0.0 copy-done.5
  22.1 0.0 copy-done.6
  22.1 0.0 copy-start.2
  22.2 2.2 %copy-done.2 = f32[1,1,16,256,256]{4,3,2,1,0:T(8,128)S(1)} copy-done((f32[1,1,16,256,256]{4,3,2,1,0:T(8,128)S(1)}, f32[1,1,16,256,256]{4,3,2,1,0:T(8,128)}, u32[]{:S(2)}) %copy-start.2) | copy-done | bytes 4194328
  24.3 2.2 %shard_map.132 = (f32[16,384]{1,0:T(8,128)S(1)}, f32[128,256]{1,0:T(8,128)S(1)}, f32[8,128]{1,0:T(8,128)S(1)}, f32[128,128]{1,0:T(8,128)S(1)}) custom-call(s32[16]{0:T(128)S(1)} %bitcast.26, s32[1]{0:T(128)} %constant.0.clone.1.refs_1_, f32[2]{0:T(128)S(1)} %pad_maximum_fusion.refs_2_.refs_1_, f32[128,384]{1,0:T(8,128)S(1)} %bitcast.20, ...), custom_call_target="tpu_custom_call" | custom-call | tf_op jit(solution)/shard_map/pallas_call | solution.py:186
  26.6 0.1 collective-permute-start.2
  26.6 1.6 %collective-permute-start.1 = (f32[16,384]{1,0:T(8,128)S(1)}, f32[16,384]{1,0:T(8,128)S(1)}, u32[]{:S(2)}, u32[]{:S(2)}) collective-permute-start(f32[16,384]{1,0:T(8,128)S(1)} %get-tuple-element.27.refs_2_), channel_id=1, source_target_pairs={{0,2},{1,3},{2,0},{3,1},{4,6},{5,7},{6,4},{7,5},{8,10},{9,11},{10,... | collective-permute-start | bytes 73736 | tf_op jit(solution)/shard_map/ppermute | solution.py:198
  28.2 0.3 collective-permute-start
  28.5 1.5 %collective-permute-start.4 = (f32[16,256]{1,0:T(8,128)S(1)}, f32[16,256]{1,0:T(8,128)S(1)}, u32[]{:S(2)}, u32[]{:S(2)}) collective-permute-start(f32[16,256]{1,0:T(8,128)S(1)} %shard_map.133.refs_6_), channel_id=1, source_target_pairs={{0,2},{1,3},{2,0},{3,1},{4,6},{5,7},{6,4},{7,5},{8,10},{9,11},{10,... | collective-permute-start | bytes 49160 | tf_op jit(solution)/shard_map/ppermute | solution.py:198
  30.0 0.0 collective-permute-done.5.refs_9_
  30.0 0.0 collective-permute-start.3
  30.0 2.2 %collective-permute-done.4.refs_8_ = f32[16,256]{1,0:T(8,128)S(1)} collective-permute-done((f32[16,256]{1,0:T(8,128)S(1)}, f32[16,256]{1,0:T(8,128)S(1)}, u32[]{:S(2)}, u32[]{:S(2)}) %collective-permute-start.4) | collective-permute-done | bytes 16416 | tf_op jit(solution)/shard_map/ppermute | solution.py:198
  32.2 0.0 collective-permute-done.3.refs_7_
  32.2 0.0 collective-permute-done.2.refs_5_
  32.2 0.0 collective-permute-done.1.refs_4_
  32.2 0.0 collective-permute-done.refs_3_
  32.2 0.0 copy-done.8
  32.3 2.0 %shard_map.134 = (f32[16,256]{1,0:T(8,128)S(1)}, f32[16,384]{1,0:T(8,128)S(1)}, f32[16,256]{1,0:T(8,128)S(1)}, f32[8,128]{1,0:T(8,128)S(1)}) custom-call(s32[16]{0:T(128)S(1)} %bitcast.27, f32[2]{0:T(128)S(1)} %pad_maximum_fusion.refs_2_.refs_1_, f32[16,384]{1,0:T(8,128)S(1)} %get-tuple-element.27.refs_2_, f32[16,384]{1,0:T(8,128)S(1)} %collective-permute-done.refs_3_, ...), custom_call_target="tpu_custom_call" | custom-call | tf_op jit(solution)/shard_map/pallas_call | solution.py:186
  34.3 12.4 %all_to_all.20 = f32[8,16,384]{2,1,0:T(8,128)S(1)} all-to-all(f32[8,16,384]{2,1,0:T(8,128)S(1)} %broadcast_in_dim.9), channel_id=1, replica_groups=mesh['row'=8,'col'=4] {'row'}, dimensions={0} | all-to-all | bytes 393216 | tf_op jit(solution)/shard_map/all_to_all | solution.py:205
  46.8 2.2 %shard_map.135 = (f32[16,384]{1,0:T(8,128)S(1)}, f32[128,256]{1,0:T(8,128)S(1)}, f32[8,128]{1,0:T(8,128)S(1)}) custom-call(s32[16]{0:T(128)S(1)} %bitcast.28, s32[1]{0:T(128)} %constant.0.clone.1.refs_1_, f32[2]{0:T(128)S(1)} %pad_maximum_fusion.refs_2_.refs_1_, f32[128,384]{1,0:T(8,128)S(1)} %bitcast.22, f32[16,256,256]{2,1,0:T(8,128)S(1)} %bitcast.14, ...), custom_call_target="tpu_custom_call" | custom-call | tf_op jit(solution)/shard_map/pallas_call | solution.py:186
  49.0 0.1 collective-permute-start.8
  49.1 0.8 collective-permute-start.7
  49.8 1.1 %collective-permute-start.6 = (f32[16,384]{1,0:T(8,128)S(1)}, f32[16,384]{1,0:T(8,128)S(1)}, u32[]{:S(2)}, u32[]{:S(2)}) collective-permute-start(f32[16,384]{1,0:T(8,128)S(1)} %get-tuple-element.33.refs_2_), channel_id=1, source_target_pairs={{0,1},{1,0},{2,3},{3,2},{4,5},{5,4},{6,7},{7,6},{8,9},{9,8},{10,11... | collective-permute-start | bytes 73736 | tf_op jit(solution)/shard_map/ppermute | solution.py:198
  50.9 1.4 %collective-permute-done.8.refs_5_ = f32[16,384]{1,0:T(8,128)S(1)} collective-permute-done((f32[16,384]{1,0:T(8,128)S(1)}, f32[16,384]{1,0:T(8,128)S(1)}, u32[]{:S(2)}, u32[]{:S(2)}) %collective-permute-start.8) | collective-permute-done | bytes 24608 | tf_op jit(solution)/shard_map/ppermute | solution.py:198
  52.3 0.7 collective-permute-done.7.refs_4_
  53.0 0.0 collective-permute-done.6.refs_3_
  53.0 2.0 %shard_map.136 = (f32[16,256]{1,0:T(8,128)S(1)}, f32[16,384]{1,0:T(8,128)S(1)}, f32[16,256]{1,0:T(8,128)S(1)}, f32[8,128]{1,0:T(8,128)S(1)}) custom-call(s32[16]{0:T(128)S(1)} %bitcast.29, f32[2]{0:T(128)S(1)} %pad_maximum_fusion.refs_2_.refs_1_, f32[16,384]{1,0:T(8,128)S(1)} %get-tuple-element.33.refs_2_, f32[16,384]{1,0:T(8,128)S(1)} %collective-permute-done.6.refs_3_, ...), custom_call_target="tpu_custom_call" | custom-call | tf_op jit(solution)/shard_map/pallas_call | solution.py:186
  55.0 11.1 %all_to_all.21 = f32[8,16,384]{2,1,0:T(8,128)S(1)} all-to-all(f32[8,16,384]{2,1,0:T(8,128)S(1)} %broadcast_in_dim.10), channel_id=1, replica_groups=mesh['row'=8,'col'=4] {'row'}, dimensions={0} | all-to-all | bytes 393216 | tf_op jit(solution)/shard_map/all_to_all | solution.py:205
  66.2 2.2 %shard_map.137 = (f32[16,384]{1,0:T(8,128)S(1)}, f32[128,256]{1,0:T(8,128)S(1)}, f32[8,128]{1,0:T(8,128)S(1)}) custom-call(s32[16]{0:T(128)S(1)} %bitcast.30, s32[1]{0:T(128)} %constant.0.clone.1.refs_1_, f32[2]{0:T(128)S(1)} %pad_maximum_fusion.refs_2_.refs_1_, f32[128,384]{1,0:T(8,128)S(1)} %bitcast.23, f32[16,256,256]{2,1,0:T(8,128)S(1)} %bitcast.16, ...), custom_call_target="tpu_custom_call" | custom-call | tf_op jit(solution)/shard_map/pallas_call | solution.py:186
  68.4 0.1 collective-permute-start.11
  68.5 0.9 collective-permute-start.10
  69.4 0.9 %collective-permute-start.9 = (f32[16,384]{1,0:T(8,128)S(1)}, f32[16,384]{1,0:T(8,128)S(1)}, u32[]{:S(2)}, u32[]{:S(2)}) collective-permute-start(f32[16,384]{1,0:T(8,128)S(1)} %get-tuple-element.40.refs_2_), channel_id=1, source_target_pairs={{0,1},{1,0},{2,3},{3,2},{4,5},{5,4},{6,7},{7,6},{8,9},{9,8},{10,11... | collective-permute-start | bytes 73736 | tf_op jit(solution)/shard_map/ppermute | solution.py:198
  70.3 1.4 %collective-permute-done.11.refs_5_ = f32[16,384]{1,0:T(8,128)S(1)} collective-permute-done((f32[16,384]{1,0:T(8,128)S(1)}, f32[16,384]{1,0:T(8,128)S(1)}, u32[]{:S(2)}, u32[]{:S(2)}) %collective-permute-start.11) | collective-permute-done | bytes 24608 | tf_op jit(solution)/shard_map/ppermute | solution.py:198
  71.7 0.8 collective-permute-done.10.refs_4_
  72.5 0.0 collective-permute-done.9.refs_3_
  72.5 2.0 %shard_map.138 = (f32[16,256]{1,0:T(8,128)S(1)}, f32[16,384]{1,0:T(8,128)S(1)}, f32[16,256]{1,0:T(8,128)S(1)}, f32[8,128]{1,0:T(8,128)S(1)}) custom-call(s32[16]{0:T(128)S(1)} %bitcast.31, f32[2]{0:T(128)S(1)} %pad_maximum_fusion.refs_2_.refs_1_, f32[16,384]{1,0:T(8,128)S(1)} %get-tuple-element.40.refs_2_, f32[16,384]{1,0:T(8,128)S(1)} %collective-permute-done.9.refs_3_, ...), custom_call_target="tpu_custom_call" | custom-call | tf_op jit(solution)/shard_map/pallas_call | solution.py:186
  74.6 11.1 %all_to_all.22 = f32[8,16,384]{2,1,0:T(8,128)S(1)} all-to-all(f32[8,16,384]{2,1,0:T(8,128)S(1)} %broadcast_in_dim.11), channel_id=1, replica_groups=mesh['row'=8,'col'=4] {'row'}, dimensions={0} | all-to-all | bytes 393216 | tf_op jit(solution)/shard_map/all_to_all | solution.py:205
  85.7 2.7 %shard_map.139 = (f32[16,384]{1,0:T(8,128)S(1)}, f32[128,256]{1,0:T(8,128)}, f32[8,128]{1,0:T(8,128)S(1)}) custom-call(s32[16]{0:T(128)S(1)} %bitcast.32, s32[1]{0:T(128)} %constant.0.clone.1.refs_1_, f32[2]{0:T(128)S(1)} %pad_maximum_fusion.refs_2_.refs_1_, f32[128,384]{1,0:T(8,128)S(1)} %bitcast.21, f32[16,256,256]{2,1,0:T(8,128)S(1)} %bitcast.18, ...), custom_call_target="tpu_custom_call" | custom-call | tf_op jit(solution)/shard_map/pallas_call | solution.py:186
  88.4 0.0 collective-permute-start.14
  88.4 1.2 %collective-permute-start.13 = (f32[16,384]{1,0:T(8,128)S(1)}, f32[16,384]{1,0:T(8,128)S(1)}, u32[]{:S(2)}, u32[]{:S(2)}) collective-permute-start(f32[16,384]{1,0:T(8,128)S(1)} %get-tuple-element.48.refs_2_), channel_id=1, source_target_pairs={{0,2},{1,3},{2,0},{3,1},{4,6},{5,7},{6,4},{7,5},{8,10},{9,11},{10,... | collective-permute-start | bytes 73736 | tf_op jit(solution)/shard_map/ppermute | solution.py:198
  89.6 0.6 collective-permute-start.12
  90.2 1.4 %collective-permute-done.14.refs_5_ = f32[16,384]{1,0:T(8,128)S(1)} collective-permute-done((f32[16,384]{1,0:T(8,128)S(1)}, f32[16,384]{1,0:T(8,128)S(1)}, u32[]{:S(2)}, u32[]{:S(2)}) %collective-permute-start.14) | collective-permute-done | bytes 24608 | tf_op jit(solution)/shard_map/ppermute | solution.py:198
  91.7 0.5 collective-permute-done.13.refs_4_
  92.2 0.0 collective-permute-done.12.refs_3_
  92.2 1.2 %shard_map.140 = f32[16,256]{1,0:T(8,128)} custom-call(s32[16]{0:T(128)S(1)} %bitcast.33, f32[2]{0:T(128)S(1)} %pad_maximum_fusion.refs_2_.refs_1_, f32[16,384]{1,0:T(8,128)S(1)} %get-tuple-element.48.refs_2_, f32[16,384]{1,0:T(8,128)S(1)} %collective-permute-done.12.refs_3_, f32[16,384]{1,0:T(8,128)S(1)} %collective-permute-done.13.refs_4_, ...), custom_call_target="tpu_custom_call" | custom-call | tf_op jit(solution)/shard_map/pallas_call | solution.py:186
  (14 shorter events, 0.1 us)
Async XLA Ops:
  0.6 13.5 %copy-start.13 = (s32[1,1,16]{2,1,0:T(1,128)S(1)}, s32[1,1,16]{2,1,0:T(1,128)}, u32[]{:S(2)}) copy-start(s32[1,1,16]{2,1,0:T(1,128)} %param.13) | copy-start | bytes 196
  0.6 2.2 %copy-start = (f32[1,1,16,256,256]{4,3,2,1,0:T(8,128)S(1)}, f32[1,1,16,256,256]{4,3,2,1,0:T(8,128)}, u32[]{:S(2)}) copy-start(f32[1,1,16,256,256]{4,3,2,1,0:T(8,128)} %param.12) | copy-start | bytes 12582916
  2.8 0.7 copy-start.10
  3.6 0.7 copy-start.12
  4.2 10.0 %copy-start.7 = (f32[128,256]{1,0:T(8,128)S(1)}, f32[128,256]{1,0:T(8,128)}, u32[]{:S(2)}) copy-start(f32[128,256]{1,0:T(8,128)} %vector_ref.1) | copy-start | bytes 393220
  4.2 17.9 %copy-start.3 = (f32[128,256]{1,0:T(8,128)S(1)}, f32[128,256]{1,0:T(8,128)}, u32[]{:S(2)}) copy-start(f32[128,256]{1,0:T(8,128)} %refs_6_.7) | copy-start | bytes 393220
  4.2 17.9 %copy-start.4 = (f32[128,256]{1,0:T(8,128)S(1)}, f32[128,256]{1,0:T(8,128)}, u32[]{:S(2)}) copy-start(f32[128,256]{1,0:T(8,128)} %refs_7_.7) | copy-start | bytes 393220
  4.2 17.9 %copy-start.5 = (f32[128,256]{1,0:T(8,128)S(1)}, f32[128,256]{1,0:T(8,128)}, u32[]{:S(2)}) copy-start(f32[128,256]{1,0:T(8,128)} %refs_8_.7) | copy-start | bytes 393220
  4.2 17.9 %copy-start.6 = (s32[128,256]{1,0:T(8,128)S(1)}, s32[128,256]{1,0:T(8,128)}, u32[]{:S(2)}) copy-start(s32[128,256]{1,0:T(8,128)} %refs_9_.7) | copy-start | bytes 393220
  6.9 15.3 %all-to-all-start = ((f32[8,16,384]{2,1,0:T(8,128)}), f32[8,16,384]{2,1,0:T(8,128)S(1)}, u32[]{:S(2)}, u32[]{:S(2)}) async-start(f32[8,16,384]{2,1,0:T(8,128)} %broadcast_in_dim.8), calls=%async_computation | async-start | bytes 393216 | tf_op jit(solution)/shard_map/all_to_all | solution.py:205
  14.2 2.2 %copy-start.1 = (f32[1,1,16,256,256]{4,3,2,1,0:T(8,128)S(1)}, f32[1,1,16,256,256]{4,3,2,1,0:T(8,128)}, u32[]{:S(2)}) copy-start(f32[1,1,16,256,256]{4,3,2,1,0:T(8,128)} %param.12) | copy-start | bytes 12582916
  16.4 15.9 %copy-start.8 = (f32[16,256]{1,0:T(8,128)S(1)}, f32[16,256]{1,0:T(8,128)}, u32[]{:S(2)}) copy-start(f32[16,256]{1,0:T(8,128)} %refs_10_.5) | copy-start | bytes 49156
  16.4 15.9 %copy-start.9 = (s32[16,256]{1,0:T(8,128)S(1)}, s32[16,256]{1,0:T(8,128)}, u32[]{:S(2)}) copy-start(s32[16,256]{1,0:T(8,128)} %refs_11_.5) | copy-start | bytes 49156
  16.4 15.9 %copy-start.11 = (f32[16,256]{1,0:T(8,128)S(1)}, f32[16,256]{1,0:T(8,128)}, u32[]{:S(2)}) copy-start(f32[16,256]{1,0:T(8,128)} %refs_12_.1) | copy-start | bytes 49156
  18.2 11.8 %collective-permute-start.5 = (f32[16,256]{1,0:T(8,128)S(1)}, f32[16,256]{1,0:T(8,128)S(1)}, u32[]{:S(2)}, u32[]{:S(2)}) collective-permute-start(f32[16,256]{1,0:T(8,128)S(1)} %shard_map.133.refs_6_), channel_id=1, source_target_pairs={{0,3},{1,2},{2,1},{3,0},{4,7},{5,6},{6,5},{7,4},{8,11},{9,10},{10,... | collective-permute-start | bytes 49160 | tf_op jit(solution)/shard_map/ppermute | solution.py:198
  22.1 2.2 %copy-start.2 = (f32[1,1,16,256,256]{4,3,2,1,0:T(8,128)S(1)}, f32[1,1,16,256,256]{4,3,2,1,0:T(8,128)}, u32[]{:S(2)}) copy-start(f32[1,1,16,256,256]{4,3,2,1,0:T(8,128)} %param.12) | copy-start | bytes 12582916
  26.6 5.7 %collective-permute-start.2 = (f32[16,384]{1,0:T(8,128)S(1)}, f32[16,384]{1,0:T(8,128)S(1)}, u32[]{:S(2)}, u32[]{:S(2)}) collective-permute-start(f32[16,384]{1,0:T(8,128)S(1)} %get-tuple-element.27.refs_2_), channel_id=1, source_target_pairs={{0,3},{1,2},{2,1},{3,0},{4,7},{5,6},{6,5},{7,4},{8,11},{9,10},{10,... | collective-permute-start | bytes 73736 | tf_op jit(solution)/shard_map/ppermute | solution.py:198
  26.6 5.6 %collective-permute-start.1 = (f32[16,384]{1,0:T(8,128)S(1)}, f32[16,384]{1,0:T(8,128)S(1)}, u32[]{:S(2)}, u32[]{:S(2)}) collective-permute-start(f32[16,384]{1,0:T(8,128)S(1)} %get-tuple-element.27.refs_2_), channel_id=1, source_target_pairs={{0,2},{1,3},{2,0},{3,1},{4,6},{5,7},{6,4},{7,5},{8,10},{9,11},{10,... | collective-permute-start | bytes 73736 | tf_op jit(solution)/shard_map/ppermute | solution.py:198
  28.2 4.0 %collective-permute-start = (f32[16,384]{1,0:T(8,128)S(1)}, f32[16,384]{1,0:T(8,128)S(1)}, u32[]{:S(2)}, u32[]{:S(2)}) collective-permute-start(f32[16,384]{1,0:T(8,128)S(1)} %get-tuple-element.27.refs_2_), channel_id=1, source_target_pairs={{0,1},{1,0},{2,3},{3,2},{4,5},{5,4},{6,7},{7,6},{8,9},{9,8},{10,11... | collective-permute-start | bytes 73736 | tf_op jit(solution)/shard_map/ppermute | solution.py:198
  28.5 3.7 %collective-permute-start.4 = (f32[16,256]{1,0:T(8,128)S(1)}, f32[16,256]{1,0:T(8,128)S(1)}, u32[]{:S(2)}, u32[]{:S(2)}) collective-permute-start(f32[16,256]{1,0:T(8,128)S(1)} %shard_map.133.refs_6_), channel_id=1, source_target_pairs={{0,2},{1,3},{2,0},{3,1},{4,6},{5,7},{6,4},{7,5},{8,10},{9,11},{10,... | collective-permute-start | bytes 49160 | tf_op jit(solution)/shard_map/ppermute | solution.py:198
  30.0 2.2 %collective-permute-start.3 = (f32[16,256]{1,0:T(8,128)S(1)}, f32[16,256]{1,0:T(8,128)S(1)}, u32[]{:S(2)}, u32[]{:S(2)}) collective-permute-start(f32[16,256]{1,0:T(8,128)S(1)} %shard_map.133.refs_6_), channel_id=1, source_target_pairs={{0,1},{1,0},{2,3},{3,2},{4,5},{5,4},{6,7},{7,6},{8,9},{9,8},{10,11... | collective-permute-start | bytes 49160 | tf_op jit(solution)/shard_map/ppermute | solution.py:198
  49.0 3.3 %collective-permute-start.8 = (f32[16,384]{1,0:T(8,128)S(1)}, f32[16,384]{1,0:T(8,128)S(1)}, u32[]{:S(2)}, u32[]{:S(2)}) collective-permute-start(f32[16,384]{1,0:T(8,128)S(1)} %get-tuple-element.33.refs_2_), channel_id=1, source_target_pairs={{0,3},{1,2},{2,1},{3,0},{4,7},{5,6},{6,5},{7,4},{8,11},{9,10},{10,... | collective-permute-start | bytes 73736 | tf_op jit(solution)/shard_map/ppermute | solution.py:198
  49.1 3.9 %collective-permute-start.7 = (f32[16,384]{1,0:T(8,128)S(1)}, f32[16,384]{1,0:T(8,128)S(1)}, u32[]{:S(2)}, u32[]{:S(2)}) collective-permute-start(f32[16,384]{1,0:T(8,128)S(1)} %get-tuple-element.33.refs_2_), channel_id=1, source_target_pairs={{0,2},{1,3},{2,0},{3,1},{4,6},{5,7},{6,4},{7,5},{8,10},{9,11},{10,... | collective-permute-start | bytes 73736 | tf_op jit(solution)/shard_map/ppermute | solution.py:198
  49.8 3.2 %collective-permute-start.6 = (f32[16,384]{1,0:T(8,128)S(1)}, f32[16,384]{1,0:T(8,128)S(1)}, u32[]{:S(2)}, u32[]{:S(2)}) collective-permute-start(f32[16,384]{1,0:T(8,128)S(1)} %get-tuple-element.33.refs_2_), channel_id=1, source_target_pairs={{0,1},{1,0},{2,3},{3,2},{4,5},{5,4},{6,7},{7,6},{8,9},{9,8},{10,11... | collective-permute-start | bytes 73736 | tf_op jit(solution)/shard_map/ppermute | solution.py:198
  68.4 3.3 %collective-permute-start.11 = (f32[16,384]{1,0:T(8,128)S(1)}, f32[16,384]{1,0:T(8,128)S(1)}, u32[]{:S(2)}, u32[]{:S(2)}) collective-permute-start(f32[16,384]{1,0:T(8,128)S(1)} %get-tuple-element.40.refs_2_), channel_id=1, source_target_pairs={{0,3},{1,2},{2,1},{3,0},{4,7},{5,6},{6,5},{7,4},{8,11},{9,10},{10,... | collective-permute-start | bytes 73736 | tf_op jit(solution)/shard_map/ppermute | solution.py:198
  68.5 4.1 %collective-permute-start.10 = (f32[16,384]{1,0:T(8,128)S(1)}, f32[16,384]{1,0:T(8,128)S(1)}, u32[]{:S(2)}, u32[]{:S(2)}) collective-permute-start(f32[16,384]{1,0:T(8,128)S(1)} %get-tuple-element.40.refs_2_), channel_id=1, source_target_pairs={{0,2},{1,3},{2,0},{3,1},{4,6},{5,7},{6,4},{7,5},{8,10},{9,11},{10,... | collective-permute-start | bytes 73736 | tf_op jit(solution)/shard_map/ppermute | solution.py:198
  69.4 3.2 %collective-permute-start.9 = (f32[16,384]{1,0:T(8,128)S(1)}, f32[16,384]{1,0:T(8,128)S(1)}, u32[]{:S(2)}, u32[]{:S(2)}) collective-permute-start(f32[16,384]{1,0:T(8,128)S(1)} %get-tuple-element.40.refs_2_), channel_id=1, source_target_pairs={{0,1},{1,0},{2,3},{3,2},{4,5},{5,4},{6,7},{7,6},{8,9},{9,8},{10,11... | collective-permute-start | bytes 73736 | tf_op jit(solution)/shard_map/ppermute | solution.py:198
  88.4 3.3 %collective-permute-start.14 = (f32[16,384]{1,0:T(8,128)S(1)}, f32[16,384]{1,0:T(8,128)S(1)}, u32[]{:S(2)}, u32[]{:S(2)}) collective-permute-start(f32[16,384]{1,0:T(8,128)S(1)} %get-tuple-element.48.refs_2_), channel_id=1, source_target_pairs={{0,3},{1,2},{2,1},{3,0},{4,7},{5,6},{6,5},{7,4},{8,11},{9,10},{10,... | collective-permute-start | bytes 73736 | tf_op jit(solution)/shard_map/ppermute | solution.py:198
  88.4 3.8 %collective-permute-start.13 = (f32[16,384]{1,0:T(8,128)S(1)}, f32[16,384]{1,0:T(8,128)S(1)}, u32[]{:S(2)}, u32[]{:S(2)}) collective-permute-start(f32[16,384]{1,0:T(8,128)S(1)} %get-tuple-element.48.refs_2_), channel_id=1, source_target_pairs={{0,2},{1,3},{2,0},{3,1},{4,6},{5,7},{6,4},{7,5},{8,10},{9,11},{10,... | collective-permute-start | bytes 73736 | tf_op jit(solution)/shard_map/ppermute | solution.py:198
  89.6 2.6 %collective-permute-start.12 = (f32[16,384]{1,0:T(8,128)S(1)}, f32[16,384]{1,0:T(8,128)S(1)}, u32[]{:S(2)}, u32[]{:S(2)}) collective-permute-start(f32[16,384]{1,0:T(8,128)S(1)} %get-tuple-element.48.refs_2_), channel_id=1, source_target_pairs={{0,1},{1,0},{2,3},{3,2},{4,5},{5,4},{6,7},{7,6},{8,9},{9,8},{10,11... | collective-permute-start | bytes 73736 | tf_op jit(solution)/shard_map/ppermute | solution.py:198

commit v2 on v1

v2 whole, which is shorter than its diff:
```python
import functools

import jax
import jax.numpy as jnp
from jax import lax
from jax.experimental import pallas as pl
from jax.experimental.pallas import tpu as pltpu
from jax.sharding import PartitionSpec as P

ITERS = 4
LANES = 128

highest = lax.Precision.HIGHEST


def square_sum(values):
    return jnp.sum(jnp.sum(values, axis=0, keepdims=True), axis=1, keepdims=True)


def columns_of(rows):
    count, width = rows.shape
    padded = jnp.concatenate([rows, jnp.zeros((128 - count, width), rows.dtype)], axis=0)
    return padded.T


def forward(tiles_ref, slots_ref, vector_ref, row_tiles, col_tiles):
    tile_count, height, width = tiles_ref.shape
    lane = lax.broadcasted_iota(jnp.int32, (height, 128), 1)

    def step(t, total):
        slot = slots_ref[t]
        picked = vector_ref[pl.ds(slot % col_tiles, 1), :]
        product = jnp.sum(tiles_ref[t] * picked, axis=1, keepdims=True)
        return total + jnp.where(lane == slot // col_tiles, product, 0.0)

    total = lax.fori_loop(0, tile_count, step, jnp.zeros((height, 128), jnp.float32), unroll=2)
    return total.T[:row_tiles]


def backward(tiles_ref, slots_ref, rows, out_ref, col_tiles):
    tile_count, height, width = tiles_ref.shape
    columns = columns_of(rows)
    lane = lax.broadcasted_iota(jnp.int32, columns.shape, 1)
    halves = width // LANES

    def step(t, carry):
        slot = slots_ref[t]
        mine = jnp.where(lane == slot // col_tiles, columns, 0.0)
        picked = jnp.sum(mine, axis=1, keepdims=True)
        product = jnp.sum(tiles_ref[t] * picked, axis=0, keepdims=True)
        for h in range(halves):
            out_ref[pl.ds(h * tile_count + t, 1), :] = product[:, h * LANES : (h + 1) * LANES]
        return carry

    lax.fori_loop(0, tile_count, step, 0, unroll=2)


def pack(out_ref, values, start=0):
    count, width = values.shape
    for h in range(width // LANES):
        block = values[:, h * LANES : (h + 1) * LANES]
        out_ref[start + h * count : start + (h + 1) * count, :] = block


def unpack(values, count, width, start=0):
    blocks = [
        values[start + h * count : start + (h + 1) * count] for h in range(width // LANES)
    ]
    return jnp.concatenate(blocks, axis=1)


def start_kernel(slots_ref, tiles_ref, dual_ref, out_ref, *, col_tiles):
    tile_count, height, width = tiles_ref.shape
    meta = tile_count * (width // LANES)
    for t in range(tile_count):
        column = slots_ref[t] % col_tiles
        out_ref[meta + t : meta + t + 1, :] = jnp.full((1, LANES), column, jnp.int32).astype(
            jnp.float32
        )
    backward(tiles_ref, slots_ref, dual_ref[...], out_ref, col_tiles)


def primal_kernel(*refs, iteration, row_tiles):
    slots_ref, scalars_ref, arrived_ref = refs[:3]
    tiles_ref, primal_ref, cost_ref, lower_ref, width_ref, kind_ref = refs[3:9]
    refs = refs[9:]
    if iteration > 0:
        hot_ref, step_ref, moved_ref = refs[:3]
        refs = refs[3:]
    out_ref, primal_out, step_out = refs[:3]
    refs = refs[3:]
    if iteration == 0:
        hot_ref = refs[0]
        refs = refs[1:]
    gather_ref = refs[0]

    col_tiles, width = primal_ref.shape
    tile_count = tiles_ref.shape[0]
    sources = arrived_ref.shape[0]
    halves = width // LANES
    meta = tile_count * halves
    for r in range(sources):
        for h in range(halves):
            gather_ref[r * tile_count : (r + 1) * tile_count, h * LANES : (h + 1) * LANES] = (
                arrived_ref[r, h * tile_count : (h + 1) * tile_count, :]
            )
    weight = scalars_ref[0:1, 0:1]
    if iteration == 0:
        number = lax.broadcasted_iota(jnp.int32, (tile_count, col_tiles), 1).astype(jnp.float32)
        for r in range(sources):
            column = arrived_ref[r, meta : meta + tile_count, :]
            hot_ref[r * tile_count : (r + 1) * tile_count, :] = (
                column[:, 0:1] == number
            ).astype(jnp.float32)
        step_size = scalars_ref[1:2, 0:1]
    else:
        sums = arrived_ref[0, meta : meta + 8, :]
        for r in range(1, sources):
            sums = sums + arrived_ref[r, meta : meta + 8, :]
        cross = sums[0:1, 0:1]
        dual_square = sums[1:2, 0:1]
        primal_square = moved_ref[0:1, 0:1]
        before = step_ref[0:1, 0:1]
        movement = 0.5 * weight * primal_square + 0.5 * dual_square / weight
        count = iteration - 1 + 11.0
        step_size = movement / jnp.maximum(
            jnp.abs(cross) / (1.0 - count ** (-0.3)),
            movement / ((1.0 + count ** (-0.6)) * before),
        )
    step_out[...] = jnp.broadcast_to(step_size, step_out.shape)
    gradient = lax.dot_general(
        hot_ref[...],
        gather_ref[...],
        (((0,), (0,)), ((), ())),
        precision=highest,
        preferred_element_type=jnp.float32,
    )
    primal = primal_ref[...]
    kind = kind_ref[...]
    lower = lower_ref[...]
    values = primal - (step_size / weight) * (cost_ref[...] - gradient)
    lifted = jnp.where(kind >= 1, jnp.maximum(values, lower), values)
    primal_next = jnp.where(kind == 2, jnp.minimum(lifted, lower + width_ref[...]), lifted)
    primal_out[...] = primal_next
    change = primal_next - primal
    rows = row_tiles * halves
    pack(out_ref, forward(tiles_ref, slots_ref, primal_out, row_tiles, col_tiles))
    out_ref[rows : rows + 8, :] = jnp.broadcast_to(square_sum(change * change), (8, LANES))
    if iteration == 0:
        pack(out_ref, forward(tiles_ref, slots_ref, primal_ref, row_tiles, col_tiles), rows + 8)


def dual_kernel(*refs, last, first, part_count, col_tiles):
    refs = list(refs)
    part_refs = refs[:part_count]
    refs = refs[part_count:]
    scalars_ref, step_ref, dual_ref, side_ref, kind_ref = refs[:5]
    refs = refs[5:]
    if not first:
        image_ref = refs.pop(0)
    if not last:
        slots_ref, tiles_ref = refs[:2]
        refs = refs[2:]
    dual_out = refs.pop(0)

    values = [ref[...] for ref in part_refs]
    while len(values) > 1:
        values = [values[i] + values[i + 1] for i in range(0, len(values), 2)]
    total = values[0]
    row_tiles, width = dual_ref.shape
    weight = scalars_ref[0:1, 0:1]
    rows = row_tiles * (width // LANES)
    image_next = unpack(total, row_tiles, width)
    image = unpack(total, row_tiles, width, rows + 8) if first else image_ref[...]
    dual = dual_ref[...]
    step_size = step_ref[0:1, 0:1]
    values = dual + (step_size * weight) * (side_ref[...] - 2.0 * image_next + image)
    dual_next = jnp.where(kind_ref[...] == 1, jnp.maximum(values, 0.0), values)
    dual_out[...] = dual_next
    if last:
        return
    out_ref, image_out, moved_out = refs[:3]
    image_out[...] = image_next
    moved_out[...] = total[rows : rows + 8]
    change = dual_next - dual
    cross = square_sum(change * (image_next - image))
    dual_square = square_sum(change * change)
    meta = tiles_ref.shape[0] * (width // LANES)
    which = lax.broadcasted_iota(jnp.int32, (8, LANES), 0)
    out_ref[meta : meta + 8, :] = jnp.where(
        which == 0, cross, jnp.where(which == 1, dual_square, 0.0)
    )
    backward(tiles_ref, slots_ref, dual_next, out_ref, col_tiles)


def call(kernel, outs, inputs, scratch=(), spaces=None):
    spaces = spaces or {}
    specs = [
        pl.BlockSpec(memory_space=spaces.get(i, pltpu.VMEM)) for i in range(len(inputs))
    ]
    return pl.pallas_call(
        kernel,
        out_shape=outs,
        in_specs=specs,
        out_specs=[pl.BlockSpec(memory_space=pltpu.VMEM) for _ in outs],
        scratch_shapes=scratch,
        compiler_params=pltpu.CompilerParams(vmem_limit_bytes=32 * 1024 * 1024),
    )(*inputs)


def exchange(values, axis, size):
    others = [
        lax.ppermute(values, axis, [(i, i ^ k) for i in range(size)]) for k in range(1, size)
    ]
    return [values] + others


def gather_rows(values, size):
    copies = jnp.broadcast_to(values[None], (size,) + values.shape)
    return lax.all_to_all(copies, "row", split_axis=0, concat_axis=0)


def shards(
    matrix_tiles,
    tile_slot,
    cost_vector,
    lower_bound,
    bound_width,
    variable_kind,
    right_side,
    row_kind,
    primal_start,
    dual_start,
    primal_weight,
    step_start,
):
    tile_set = matrix_tiles[0, 0]
    slots = tile_slot[0, 0]
    row_tiles, width = right_side.shape
    col_tiles = cost_vector.shape[0]
    tile_count = slots.shape[0]
    row_count = lax.axis_size("row")
    col_count = lax.axis_size("col")
    scalars = jnp.where(
        lax.broadcasted_iota(jnp.int32, (8, LANES), 0) == 0, primal_weight, step_start
    )
    smem = pltpu.SMEM
    halves = width // LANES

    def array(*shape):
        return jax.ShapeDtypeStruct(shape, jnp.float32)

    (sent,) = call(
        functools.partial(start_kernel, col_tiles=col_tiles),
        [array(tile_count * (halves + 1), LANES)],
        [slots, tile_set, dual_start],
        spaces={0: smem},
    )
    primal, dual = primal_start, dual_start
    hot = step_size = moved = image = None
    for iteration in range(ITERS):
        first, last = iteration == 0, iteration + 1 == ITERS
        arrived = gather_rows(sent, row_count)
        sources = row_count * tile_count
        rows = row_tiles * halves
        outs = [
            array(rows + 8 + (rows if first else 0), LANES),
            array(*primal.shape),
            array(8, LANES),
        ]
        inputs = [slots, scalars, arrived, tile_set, primal]
        inputs += [cost_vector, lower_bound, bound_width, variable_kind]
        if first:
            outs.append(array(sources, col_tiles))
        else:
            inputs += [hot, step_size, moved]
        results = call(
            functools.partial(primal_kernel, iteration=iteration, row_tiles=row_tiles),
            outs,
            inputs,
            scratch=[pltpu.VMEM((sources, width), jnp.float32)],
            spaces={0: smem},
        )
        image_part, primal, step_size = results[:3]
        if first:
            hot = results[3]
        parts = exchange(image_part, "col", col_count)
        outs = [array(*dual.shape)]
        inputs = [*parts, scalars, step_size, dual, right_side, row_kind]
        spaces = {}
        if not first:
            inputs.append(image)
        if not last:
            spaces[len(inputs)] = smem
            inputs += [slots, tile_set]
            outs += [array(tile_count * halves + 8, LANES), array(*dual.shape), array(8, LANES)]
        results = call(
            functools.partial(
                dual_kernel, last=last, first=first, part_count=len(parts), col_tiles=col_tiles
            ),
            outs,
            inputs,
            spaces=spaces,
        )
        dual = results[0]
        if not last:
            sent, image, moved = results[1:]
    return (primal, dual)


def solution(mesh):
    return jax.shard_map(
        shards,
        mesh=mesh,
        in_specs=(
            P("row", "col", None, None, None),
            P("row", "col", None),
            P("col", None),
            P("col", None),
            P("col", None),
            P("col", None),
            P("row", None),
            P("row", None),
            P("col", None),
            P("row", None),
            P(),
            P(),
        ),
        out_specs=(P("col", None), P("row", None)),
        check_vma=False,
    )
```

time: 93.9 us -> 90.8 us (0.967)
  waiting for transfers between devices: 10.4 us -> 15.1 us
  starting transfers between devices: 17.1 us -> 14.9 us
  local copies, waits for them, and re-layouts: 8.69 us -> 6.57 us
  blocking collectives: 34.7 us -> 32.7 us
  Pallas kernels: 20.4 us -> 19 us
    all_to_all x1, waiting for transfers between devices: 1.87 us -> 6.64 us  [gather_rows(): return lax.all_to_all(copies, 'row', split_axis=0, concat_axis=0)]
    unnamed x28 -> x26, local copies, waits for them, and re-layouts: 7.96 us -> 5.78 us
    ppermute x15 -> x12, starting transfers between devices: 9.74 us -> 7.59 us  [exchange(): lax.ppermute(values, axis, [(i, i ^ k) for i in range(size)])]
    all_to_all x3, blocking collectives: 34.7 us -> 32.7 us  [gather_rows(): return lax.all_to_all(copies, 'row', split_axis=0, concat_axis=0)]
    pallas_call x10 -> x9, Pallas kernels: 20.4 us -> 19 us  [call(): pl.pallas_call(kernel, out_shape=outs, in_specs=specs, out_specs=[pl.Bloc...]
    ppermute x15 -> x12, waiting for transfers between devices: 8.5 us -> 8.42 us  [exchange(): lax.ppermute(values, axis, [(i, i ^ k) for i in range(size)])]
  transfers between devices with their start and end apart: 16 -> 13, of which waited for: 8 -> 9; matrix products, arithmetic and copies ran while one was open for 0% -> 0% of each run, Pallas kernels for 4% -> 0%
where the time goes in v2:
time: 90.8 us; the launch traced here: 90.3 us
  blocking collectives  32.7 us (36%)
  Pallas kernels  19 us (21%)
  waiting for transfers between devices  15.1 us (17%)
  starting transfers between devices  14.9 us (16%)
  local copies, waits for them, and re-layouts  6.57 us (7%)
  between operations  2.11 us (2%)
    all_to_all x3, blocking collectives, gather_rows(): return lax.all_to_all(copies, 'row', split_axis=0, concat_axis=0)  32.7 us
    pallas_call x9, Pallas kernels, call(): pl.pallas_call(kernel, out_shape=outs, in_specs=specs, out_specs=[pl.Bloc...  19 us
    ppermute x12, waiting for transfers between devices, exchange(): lax.ppermute(values, axis, [(i, i ^ k) for i in range(size)])  8.42 us
    ppermute x12, starting transfers between devices, exchange(): lax.ppermute(values, axis, [(i, i ^ k) for i in range(size)])  7.59 us
    all_to_all x1, starting transfers between devices, gather_rows(): return lax.all_to_all(copies, 'row', split_axis=0, concat_axis=0)  7.31 us
    all_to_all x1, waiting for transfers between devices, gather_rows(): return lax.all_to_all(copies, 'row', split_axis=0, concat_axis=0)  6.64 us
    unnamed x26, local copies, waits for them, and re-layouts  5.78 us
  transfers between devices with their start and end apart: 13, of which 9 were waited for; matrix products, arithmetic and copies ran while one was open for 0% of the time, Pallas kernels for 0%

profile of v2, /device:TPU:0, one launch (start us, length us, event | category | flops | bytes accessed | tf_op | source)
XLA Modules:
  0.0 90.3 jit_solution(15636636113429007892)
XLA Ops:
  0.6 0.0 copy-start.12
  0.6 0.0 copy-start
  0.7 2.2 %copy-done = f32[1,1,16,256,256]{4,3,2,1,0:T(8,128)S(1)} copy-done((f32[1,1,16,256,256]{4,3,2,1,0:T(8,128)S(1)}, f32[1,1,16,256,256]{4,3,2,1,0:T(8,128)}, u32[]{:S(2)}) %copy-start) | copy-done | bytes 4194328
  2.8 0.0 copy-start.9
  2.8 0.7 copy-done.9
  3.6 0.0 copy-start.11
  3.6 0.7 copy-done.11
  4.2 0.0 copy-start.3
  4.2 0.0 copy-start.4
  4.2 0.0 copy-start.8
  4.2 0.0 copy-start.6
  4.2 0.0 copy-start.7
  4.3 0.0 copy-start.10
  4.3 1.9 %shard_map.131 = f32[48,128]{1,0:T(8,128)S(1)} custom-call(s32[16]{0:T(128)S(1)} %bitcast.10, f32[16,256,256]{2,1,0:T(8,128)S(1)} %bitcast.2, f32[16,256]{1,0:T(8,128)S(1)} %copy-done.9), custom_call_target="tpu_custom_call" | custom-call | tf_op jit(solution)/shard_map/pallas_call | solution.py:201
  6.2 0.7 broadcast_in_dim.18
  6.9 7.3 %all-to-all-start = ((f32[8,48,128]{2,1,0:T(8,128)}), f32[8,48,128]{2,1,0:T(8,128)S(1)}, u32[]{:S(2)}, u32[]{:S(2)}) async-start(f32[8,48,128]{2,1,0:T(8,128)} %broadcast_in_dim.18), calls=%async_computation | async-start | bytes 393216 | tf_op jit(solution)/shard_map/all_to_all | solution.py:220
  15.5 6.6 %all-to-all-done.refs_2_ = f32[8,48,128]{2,1,0:T(8,128)S(1)} async-done(((f32[8,48,128]{2,1,0:T(8,128)}), f32[8,48,128]{2,1,0:T(8,128)S(1)}, u32[]{:S(2)}, u32[]{:S(2)}) %all-to-all-start) | async-done | bytes 196640 | tf_op jit(solution)/shard_map/all_to_all | solution.py:220
  22.1 0.1 iota.7.refs_1_.refs_4_
  22.2 0.0 copy-done.12
  22.2 0.0 copy-done.2
  22.2 0.0 copy-done.3
  22.2 0.0 copy-done.4
  22.2 0.0 copy-done.5
  22.2 0.0 copy-done.8
  22.2 0.0 copy-start.1
  22.2 2.2 %copy-done.1 = f32[1,1,16,256,256]{4,3,2,1,0:T(8,128)S(1)} copy-done((f32[1,1,16,256,256]{4,3,2,1,0:T(8,128)S(1)}, f32[1,1,16,256,256]{4,3,2,1,0:T(8,128)}, u32[]{:S(2)}) %copy-start.1) | copy-done | bytes 4194328
  24.4 3.5 %shard_map.132 = (f32[72,128]{1,0:T(8,128)S(1)}, f32[128,256]{1,0:T(8,128)S(1)}, f32[8,128]{1,0:T(8,128)S(1)}, f32[128,128]{1,0:T(8,128)S(1)}) custom-call(s32[16]{0:T(128)S(1)} %bitcast.11, f32[8,128]{1,0:T(8,128)S(1)} %iota.7.refs_1_.refs_4_, f32[8,48,128]{2,1,0:T(8,128)S(1)} %all-to-all-done.refs_2_, f32[16,256,256]{2,1,0:T(8,128)S(1)} %bitcast.3, ...), custom_call_target="tpu_custom_call" | custom-call | tf_op jit(solution)/shard_map/pallas_call | solution.py:201
  28.0 0.1 collective-permute-start.2
  28.0 1.6 %collective-permute-start.1 = (f32[72,128]{1,0:T(8,128)S(1)}, f32[72,128]{1,0:T(8,128)S(1)}, u32[]{:S(2)}, u32[]{:S(2)}) collective-permute-start(f32[72,128]{1,0:T(8,128)S(1)} %get-tuple-element.27.refs_0_), channel_id=1, source_target_pairs={{0,2},{1,3},{2,0},{3,1},{4,6},{5,7},{6,4},{7,5},{8,10},{9,11},{10,... | collective-permute-start | bytes 110600 | tf_op jit(solution)/shard_map/ppermute | solution.py:213
  29.6 0.3 collective-permute-start
  29.9 1.9 %collective-permute-done.2.refs_3_ = f32[72,128]{1,0:T(8,128)S(1)} collective-permute-done((f32[72,128]{1,0:T(8,128)S(1)}, f32[72,128]{1,0:T(8,128)S(1)}, u32[]{:S(2)}, u32[]{:S(2)}) %collective-permute-start.2) | collective-permute-done | bytes 36896 | tf_op jit(solution)/shard_map/ppermute | solution.py:213
  31.7 0.4 collective-permute-done.1.refs_2_
  32.2 0.0 collective-permute-done.refs_1_
  32.2 0.0 copy-done.6
  32.2 0.0 copy-done.7
  32.2 0.0 copy-done.10
  32.2 2.0 %shard_map.133 = (f32[16,256]{1,0:T(8,128)S(1)}, f32[40,128]{1,0:T(8,128)S(1)}, f32[16,256]{1,0:T(8,128)S(1)}, f32[8,128]{1,0:T(8,128)S(1)}) custom-call(f32[72,128]{1,0:T(8,128)S(1)} %get-tuple-element.27.refs_0_, f32[72,128]{1,0:T(8,128)S(1)} %collective-permute-done.refs_1_, f32[72,128]{1,0:T(8,128)S(1)} %collective-permute-done.1.refs_2_, ...), custom_call_target="tpu_custom_call" | custom-call | tf_op jit(solution)/shard_map/pallas_call | solution.py:201
  34.2 11.5 %all_to_all.20.refs_2_ = f32[8,40,128]{2,1,0:T(8,128)S(1)} all-to-all(f32[8,40,128]{2,1,0:T(8,128)S(1)} %broadcast_in_dim.19), channel_id=1, replica_groups=mesh['row'=8,'col'=4] {'row'}, dimensions={0} | all-to-all | bytes 327680 | tf_op jit(solution)/shard_map/all_to_all | solution.py:220
  45.7 2.2 %shard_map.134 = (f32[40,128]{1,0:T(8,128)S(1)}, f32[128,256]{1,0:T(8,128)S(1)}, f32[8,128]{1,0:T(8,128)S(1)}) custom-call(s32[16]{0:T(128)S(1)} %bitcast.13, f32[8,128]{1,0:T(8,128)S(1)} %iota.7.refs_1_.refs_4_, f32[8,40,128]{2,1,0:T(8,128)S(1)} %all_to_all.20.refs_2_, f32[16,256,256]{2,1,0:T(8,128)S(1)} %bitcast.5, ...), custom_call_target="tpu_custom_call" | custom-call | tf_op jit(solution)/shard_map/pallas_call | solution.py:201
  47.9 0.1 collective-permute-start.5
  47.9 0.9 collective-permute-start.4
  48.8 1.0 %collective-permute-start.3 = (f32[40,128]{1,0:T(8,128)S(1)}, f32[40,128]{1,0:T(8,128)S(1)}, u32[]{:S(2)}, u32[]{:S(2)}) collective-permute-start(f32[40,128]{1,0:T(8,128)S(1)} %get-tuple-element.33.refs_0_), channel_id=1, source_target_pairs={{0,1},{1,0},{2,3},{3,2},{4,5},{5,4},{6,7},{7,6},{8,9},{9,8},{10,11... | collective-permute-start | bytes 61448 | tf_op jit(solution)/shard_map/ppermute | solution.py:213
  49.8 1.3 %collective-permute-done.5.refs_3_ = f32[40,128]{1,0:T(8,128)S(1)} collective-permute-done((f32[40,128]{1,0:T(8,128)S(1)}, f32[40,128]{1,0:T(8,128)S(1)}, u32[]{:S(2)}, u32[]{:S(2)}) %collective-permute-start.5) | collective-permute-done | bytes 20512 | tf_op jit(solution)/shard_map/ppermute | solution.py:213
  51.1 0.7 collective-permute-done.4.refs_2_
  51.8 0.0 collective-permute-done.3.refs_1_
  51.9 2.0 %shard_map.135 = (f32[16,256]{1,0:T(8,128)S(1)}, f32[40,128]{1,0:T(8,128)S(1)}, f32[16,256]{1,0:T(8,128)S(1)}, f32[8,128]{1,0:T(8,128)S(1)}) custom-call(f32[40,128]{1,0:T(8,128)S(1)} %get-tuple-element.33.refs_0_, f32[40,128]{1,0:T(8,128)S(1)} %collective-permute-done.3.refs_1_, f32[40,128]{1,0:T(8,128)S(1)} %collective-permute-done.4.refs_2_, ...), custom_call_target="tpu_custom_call" | custom-call | tf_op jit(solution)/shard_map/pallas_call | solution.py:201
  53.9 10.3 %all_to_all.21.refs_2_ = f32[8,40,128]{2,1,0:T(8,128)S(1)} all-to-all(f32[8,40,128]{2,1,0:T(8,128)S(1)} %broadcast_in_dim.36), channel_id=1, replica_groups=mesh['row'=8,'col'=4] {'row'}, dimensions={0} | all-to-all | bytes 327680 | tf_op jit(solution)/shard_map/all_to_all | solution.py:220
  64.2 2.2 %shard_map.136 = (f32[40,128]{1,0:T(8,128)S(1)}, f32[128,256]{1,0:T(8,128)S(1)}, f32[8,128]{1,0:T(8,128)S(1)}) custom-call(s32[16]{0:T(128)S(1)} %bitcast.15, f32[8,128]{1,0:T(8,128)S(1)} %iota.7.refs_1_.refs_4_, f32[8,40,128]{2,1,0:T(8,128)S(1)} %all_to_all.21.refs_2_, f32[16,256,256]{2,1,0:T(8,128)S(1)} %bitcast.7, ...), custom_call_target="tpu_custom_call" | custom-call | tf_op jit(solution)/shard_map/pallas_call | solution.py:201
  66.4 0.1 collective-permute-start.8
  66.4 1.3 %collective-permute-start.7 = (f32[40,128]{1,0:T(8,128)S(1)}, f32[40,128]{1,0:T(8,128)S(1)}, u32[]{:S(2)}, u32[]{:S(2)}) collective-permute-start(f32[40,128]{1,0:T(8,128)S(1)} %get-tuple-element.40.refs_0_), channel_id=1, source_target_pairs={{0,2},{1,3},{2,0},{3,1},{4,6},{5,7},{6,4},{7,5},{8,10},{9,11},{10,... | collective-permute-start | bytes 61448 | tf_op jit(solution)/shard_map/ppermute | solution.py:213
  67.8 0.5 collective-permute-start.6
  68.3 1.4 %collective-permute-done.8.refs_3_ = f32[40,128]{1,0:T(8,128)S(1)} collective-permute-done((f32[40,128]{1,0:T(8,128)S(1)}, f32[40,128]{1,0:T(8,128)S(1)}, u32[]{:S(2)}, u32[]{:S(2)}) %collective-permute-start.8) | collective-permute-done | bytes 20512 | tf_op jit(solution)/shard_map/ppermute | solution.py:213
  69.7 0.6 collective-permute-done.7.refs_2_
  70.3 0.0 collective-permute-done.6.refs_1_
  70.3 2.0 %shard_map.137 = (f32[16,256]{1,0:T(8,128)S(1)}, f32[40,128]{1,0:T(8,128)S(1)}, f32[16,256]{1,0:T(8,128)S(1)}, f32[8,128]{1,0:T(8,128)S(1)}) custom-call(f32[40,128]{1,0:T(8,128)S(1)} %get-tuple-element.40.refs_0_, f32[40,128]{1,0:T(8,128)S(1)} %collective-permute-done.6.refs_1_, f32[40,128]{1,0:T(8,128)S(1)} %collective-permute-done.7.refs_2_, ...), custom_call_target="tpu_custom_call" | custom-call | tf_op jit(solution)/shard_map/pallas_call | solution.py:201
  72.3 10.9 %all_to_all.22.refs_2_ = f32[8,40,128]{2,1,0:T(8,128)S(1)} all-to-all(f32[8,40,128]{2,1,0:T(8,128)S(1)} %broadcast_in_dim.37), channel_id=1, replica_groups=mesh['row'=8,'col'=4] {'row'}, dimensions={0} | all-to-all | bytes 327680 | tf_op jit(solution)/shard_map/all_to_all | solution.py:220
  83.2 2.6 %shard_map.138 = (f32[40,128]{1,0:T(8,128)S(1)}, f32[128,256]{1,0:T(8,128)}, f32[8,128]{1,0:T(8,128)S(1)}) custom-call(s32[16]{0:T(128)S(1)} %bitcast.17, f32[8,128]{1,0:T(8,128)S(1)} %iota.7.refs_1_.refs_4_, f32[8,40,128]{2,1,0:T(8,128)S(1)} %all_to_all.22.refs_2_, f32[16,256,256]{2,1,0:T(8,128)S(1)} %bitcast.9, f32[128,256]{1,0:T(8,128)S(1)} %get-tuple-element.45.refs_4_, ...), custom_call_target="tpu_custom_call" | custom-call | tf_op jit(solution)/shard_map/pallas_call | solution.py:201
  85.8 0.0 collective-permute-start.11
  85.8 0.7 collective-permute-start.10
  86.5 1.1 %collective-permute-start.9 = (f32[40,128]{1,0:T(8,128)S(1)}, f32[40,128]{1,0:T(8,128)S(1)}, u32[]{:S(2)}, u32[]{:S(2)}) collective-permute-start(f32[40,128]{1,0:T(8,128)S(1)} %get-tuple-element.48.refs_0_), channel_id=1, source_target_pairs={{0,1},{1,0},{2,3},{3,2},{4,5},{5,4},{6,7},{7,6},{8,9},{9,8},{10,11... | collective-permute-start | bytes 61448 | tf_op jit(solution)/shard_map/ppermute | solution.py:213
  87.7 1.3 %collective-permute-done.11.refs_3_ = f32[40,128]{1,0:T(8,128)S(1)} collective-permute-done((f32[40,128]{1,0:T(8,128)S(1)}, f32[40,128]{1,0:T(8,128)S(1)}, u32[]{:S(2)}, u32[]{:S(2)}) %collective-permute-start.11) | collective-permute-done | bytes 20512 | tf_op jit(solution)/shard_map/ppermute | solution.py:213
  89.0 0.7 collective-permute-done.10.refs_2_
  89.7 0.0 collective-permute-done.9.refs_1_
  89.7 0.6 shard_map.139
  (6 shorter events, 0.0 us)
Async XLA Ops:
  0.6 21.6 %copy-start.12 = (s32[1,1,16]{2,1,0:T(1,128)S(1)}, s32[1,1,16]{2,1,0:T(1,128)}, u32[]{:S(2)}) copy-start(s32[1,1,16]{2,1,0:T(1,128)} %param.13) | copy-start | bytes 196
  0.6 2.2 %copy-start = (f32[1,1,16,256,256]{4,3,2,1,0:T(8,128)S(1)}, f32[1,1,16,256,256]{4,3,2,1,0:T(8,128)}, u32[]{:S(2)}) copy-start(f32[1,1,16,256,256]{4,3,2,1,0:T(8,128)} %param.12) | copy-start | bytes 12582916
  2.8 0.7 copy-start.9
  3.6 0.7 copy-start.11
  4.2 18.0 %copy-start.2 = (f32[128,256]{1,0:T(8,128)S(1)}, f32[128,256]{1,0:T(8,128)}, u32[]{:S(2)}) copy-start(f32[128,256]{1,0:T(8,128)} %refs_5_.7) | copy-start | bytes 393220
  4.2 18.0 %copy-start.3 = (f32[128,256]{1,0:T(8,128)S(1)}, f32[128,256]{1,0:T(8,128)}, u32[]{:S(2)}) copy-start(f32[128,256]{1,0:T(8,128)} %refs_6_.9) | copy-start | bytes 393220
  4.2 18.0 %copy-start.4 = (f32[128,256]{1,0:T(8,128)S(1)}, f32[128,256]{1,0:T(8,128)}, u32[]{:S(2)}) copy-start(f32[128,256]{1,0:T(8,128)} %refs_7_.14) | copy-start | bytes 393220
  4.2 18.0 %copy-start.5 = (s32[128,256]{1,0:T(8,128)S(1)}, s32[128,256]{1,0:T(8,128)}, u32[]{:S(2)}) copy-start(s32[128,256]{1,0:T(8,128)} %refs_8_.14) | copy-start | bytes 393220
  4.2 18.0 %copy-start.8 = (f32[128,256]{1,0:T(8,128)S(1)}, f32[128,256]{1,0:T(8,128)}, u32[]{:S(2)}) copy-start(f32[128,256]{1,0:T(8,128)} %refs_4_.1) | copy-start | bytes 393220
  4.2 27.9 %copy-start.6 = (f32[16,256]{1,0:T(8,128)S(1)}, f32[16,256]{1,0:T(8,128)}, u32[]{:S(2)}) copy-start(f32[16,256]{1,0:T(8,128)} %refs_7_.15) | copy-start | bytes 49156
  4.2 27.9 %copy-start.7 = (s32[16,256]{1,0:T(8,128)S(1)}, s32[16,256]{1,0:T(8,128)}, u32[]{:S(2)}) copy-start(s32[16,256]{1,0:T(8,128)} %refs_8_.15) | copy-start | bytes 49156
  4.3 27.9 %copy-start.10 = (f32[16,256]{1,0:T(8,128)S(1)}, f32[16,256]{1,0:T(8,128)}, u32[]{:S(2)}) copy-start(f32[16,256]{1,0:T(8,128)} %refs_6_.6) | copy-start | bytes 49156
  6.9 15.3 %all-to-all-start = ((f32[8,48,128]{2,1,0:T(8,128)}), f32[8,48,128]{2,1,0:T(8,128)S(1)}, u32[]{:S(2)}, u32[]{:S(2)}) async-start(f32[8,48,128]{2,1,0:T(8,128)} %broadcast_in_dim.18), calls=%async_computation | async-start | bytes 393216 | tf_op jit(solution)/shard_map/all_to_all | solution.py:220
  22.2 2.2 %copy-start.1 = (f32[1,1,16,256,256]{4,3,2,1,0:T(8,128)S(1)}, f32[1,1,16,256,256]{4,3,2,1,0:T(8,128)}, u32[]{:S(2)}) copy-start(f32[1,1,16,256,256]{4,3,2,1,0:T(8,128)} %param.12) | copy-start | bytes 12582916
  28.0 3.8 %collective-permute-start.2 = (f32[72,128]{1,0:T(8,128)S(1)}, f32[72,128]{1,0:T(8,128)S(1)}, u32[]{:S(2)}, u32[]{:S(2)}) collective-permute-start(f32[72,128]{1,0:T(8,128)S(1)} %get-tuple-element.27.refs_0_), channel_id=1, source_target_pairs={{0,3},{1,2},{2,1},{3,0},{4,7},{5,6},{6,5},{7,4},{8,11},{9,10},{10,... | collective-permute-start | bytes 110600 | tf_op jit(solution)/shard_map/ppermute | solution.py:213
  28.0 4.2 %collective-permute-start.1 = (f32[72,128]{1,0:T(8,128)S(1)}, f32[72,128]{1,0:T(8,128)S(1)}, u32[]{:S(2)}, u32[]{:S(2)}) collective-permute-start(f32[72,128]{1,0:T(8,128)S(1)} %get-tuple-element.27.refs_0_), channel_id=1, source_target_pairs={{0,2},{1,3},{2,0},{3,1},{4,6},{5,7},{6,4},{7,5},{8,10},{9,11},{10,... | collective-permute-start | bytes 110600 | tf_op jit(solution)/shard_map/ppermute | solution.py:213
  29.6 2.6 %collective-permute-start = (f32[72,128]{1,0:T(8,128)S(1)}, f32[72,128]{1,0:T(8,128)S(1)}, u32[]{:S(2)}, u32[]{:S(2)}) collective-permute-start(f32[72,128]{1,0:T(8,128)S(1)} %get-tuple-element.27.refs_0_), channel_id=1, source_target_pairs={{0,1},{1,0},{2,3},{3,2},{4,5},{5,4},{6,7},{7,6},{8,9},{9,8},{10,11... | collective-permute-start | bytes 110600 | tf_op jit(solution)/shard_map/ppermute | solution.py:213
  47.9 3.3 %collective-permute-start.5 = (f32[40,128]{1,0:T(8,128)S(1)}, f32[40,128]{1,0:T(8,128)S(1)}, u32[]{:S(2)}, u32[]{:S(2)}) collective-permute-start(f32[40,128]{1,0:T(8,128)S(1)} %get-tuple-element.33.refs_0_), channel_id=1, source_target_pairs={{0,3},{1,2},{2,1},{3,0},{4,7},{5,6},{6,5},{7,4},{8,11},{9,10},{10,... | collective-permute-start | bytes 61448 | tf_op jit(solution)/shard_map/ppermute | solution.py:213
  47.9 3.9 %collective-permute-start.4 = (f32[40,128]{1,0:T(8,128)S(1)}, f32[40,128]{1,0:T(8,128)S(1)}, u32[]{:S(2)}, u32[]{:S(2)}) collective-permute-start(f32[40,128]{1,0:T(8,128)S(1)} %get-tuple-element.33.refs_0_), channel_id=1, source_target_pairs={{0,2},{1,3},{2,0},{3,1},{4,6},{5,7},{6,4},{7,5},{8,10},{9,11},{10,... | collective-permute-start | bytes 61448 | tf_op jit(solution)/shard_map/ppermute | solution.py:213
  48.8 3.1 %collective-permute-start.3 = (f32[40,128]{1,0:T(8,128)S(1)}, f32[40,128]{1,0:T(8,128)S(1)}, u32[]{:S(2)}, u32[]{:S(2)}) collective-permute-start(f32[40,128]{1,0:T(8,128)S(1)} %get-tuple-element.33.refs_0_), channel_id=1, source_target_pairs={{0,1},{1,0},{2,3},{3,2},{4,5},{5,4},{6,7},{7,6},{8,9},{9,8},{10,11... | collective-permute-start | bytes 61448 | tf_op jit(solution)/shard_map/ppermute | solution.py:213
  66.4 3.3 %collective-permute-start.8 = (f32[40,128]{1,0:T(8,128)S(1)}, f32[40,128]{1,0:T(8,128)S(1)}, u32[]{:S(2)}, u32[]{:S(2)}) collective-permute-start(f32[40,128]{1,0:T(8,128)S(1)} %get-tuple-element.40.refs_0_), channel_id=1, source_target_pairs={{0,3},{1,2},{2,1},{3,0},{4,7},{5,6},{6,5},{7,4},{8,11},{9,10},{10,... | collective-permute-start | bytes 61448 | tf_op jit(solution)/shard_map/ppermute | solution.py:213
  66.4 3.8 %collective-permute-start.7 = (f32[40,128]{1,0:T(8,128)S(1)}, f32[40,128]{1,0:T(8,128)S(1)}, u32[]{:S(2)}, u32[]{:S(2)}) collective-permute-start(f32[40,128]{1,0:T(8,128)S(1)} %get-tuple-element.40.refs_0_), channel_id=1, source_target_pairs={{0,2},{1,3},{2,0},{3,1},{4,6},{5,7},{6,4},{7,5},{8,10},{9,11},{10,... | collective-permute-start | bytes 61448 | tf_op jit(solution)/shard_map/ppermute | solution.py:213
  67.8 2.5 %collective-permute-start.6 = (f32[40,128]{1,0:T(8,128)S(1)}, f32[40,128]{1,0:T(8,128)S(1)}, u32[]{:S(2)}, u32[]{:S(2)}) collective-permute-start(f32[40,128]{1,0:T(8,128)S(1)} %get-tuple-element.40.refs_0_), channel_id=1, source_target_pairs={{0,1},{1,0},{2,3},{3,2},{4,5},{5,4},{6,7},{7,6},{8,9},{9,8},{10,11... | collective-permute-start | bytes 61448 | tf_op jit(solution)/shard_map/ppermute | solution.py:213
  85.8 3.2 %collective-permute-start.11 = (f32[40,128]{1,0:T(8,128)S(1)}, f32[40,128]{1,0:T(8,128)S(1)}, u32[]{:S(2)}, u32[]{:S(2)}) collective-permute-start(f32[40,128]{1,0:T(8,128)S(1)} %get-tuple-element.48.refs_0_), channel_id=1, source_target_pairs={{0,3},{1,2},{2,1},{3,0},{4,7},{5,6},{6,5},{7,4},{8,11},{9,10},{10,... | collective-permute-start | bytes 61448 | tf_op jit(solution)/shard_map/ppermute | solution.py:213
  85.8 3.9 %collective-permute-start.10 = (f32[40,128]{1,0:T(8,128)S(1)}, f32[40,128]{1,0:T(8,128)S(1)}, u32[]{:S(2)}, u32[]{:S(2)}) collective-permute-start(f32[40,128]{1,0:T(8,128)S(1)} %get-tuple-element.48.refs_0_), channel_id=1, source_target_pairs={{0,2},{1,3},{2,0},{3,1},{4,6},{5,7},{6,4},{7,5},{8,10},{9,11},{10,... | collective-permute-start | bytes 61448 | tf_op jit(solution)/shard_map/ppermute | solution.py:213
  86.5 3.1 %collective-permute-start.9 = (f32[40,128]{1,0:T(8,128)S(1)}, f32[40,128]{1,0:T(8,128)S(1)}, u32[]{:S(2)}, u32[]{:S(2)}) collective-permute-start(f32[40,128]{1,0:T(8,128)S(1)} %get-tuple-element.48.refs_0_), channel_id=1, source_target_pairs={{0,1},{1,0},{2,3},{3,2},{4,5},{5,4},{6,7},{7,6},{8,9},{9,8},{10,11... | collective-permute-start | bytes 61448 | tf_op jit(solution)/shard_map/ppermute | solution.py:213

commit v3 on v2

--- a/solution.py
+++ b/solution.py
@@ -37,7 +37,7 @@
     return total.T[:row_tiles]
 
 
-def backward(tiles_ref, slots_ref, rows, out_ref, col_tiles):
+def backward(tiles_ref, slots_ref, rows, out_ref, col_tiles, ready=None):
     tile_count, height, width = tiles_ref.shape
     columns = columns_of(rows)
     lane = lax.broadcasted_iota(jnp.int32, columns.shape, 1)
@@ -45,6 +45,8 @@
 
     def step(t, carry):
         slot = slots_ref[t]
+        if ready is not None:
+            ready(t)
         mine = jnp.where(lane == slot // col_tiles, columns, 0.0)
         picked = jnp.sum(mine, axis=1, keepdims=True)
         product = jnp.sum(tiles_ref[t] * picked, axis=0, keepdims=True)
@@ -69,15 +71,50 @@
     return jnp.concatenate(blocks, axis=1)
 
 
-def start_kernel(slots_ref, tiles_ref, dual_ref, out_ref, *, col_tiles):
+def start_kernel(
+    slots_hbm,
+    tiles_hbm,
+    dual_hbm,
+    weight_ref,
+    step_ref,
+    out_ref,
+    scalars_out,
+    slots_ref,
+    tiles_ref,
+    dual_ref,
+    sems,
+    *,
+    col_tiles,
+):
     tile_count, height, width = tiles_ref.shape
+
+    def tile_copy(t):
+        return pltpu.make_async_copy(tiles_hbm.at[t], tiles_ref.at[t], sems.at[t])
+
+    slots_copy = pltpu.make_async_copy(slots_hbm, slots_ref, sems.at[tile_count])
+    dual_copy = pltpu.make_async_copy(dual_hbm, dual_ref, sems.at[tile_count + 1])
+    slots_copy.start()
+    dual_copy.start()
+    for t in range(tile_count):
+        tile_copy(t).start()
+    which = lax.broadcasted_iota(jnp.int32, scalars_out.shape, 0)
+    scalars_out[...] = jnp.where(which == 0, weight_ref[0], step_ref[0])
+    slots_copy.wait()
     meta = tile_count * (width // LANES)
     for t in range(tile_count):
         column = slots_ref[t] % col_tiles
         out_ref[meta + t : meta + t + 1, :] = jnp.full((1, LANES), column, jnp.int32).astype(
             jnp.float32
         )
-    backward(tiles_ref, slots_ref, dual_ref[...], out_ref, col_tiles)
+    dual_copy.wait()
+    backward(
+        tiles_ref,
+        slots_ref,
+        dual_ref[...],
+        out_ref,
+        col_tiles,
+        ready=lambda t: tile_copy(t).wait(),
+    )
 
 
 def primal_kernel(*refs, iteration, row_tiles):
@@ -241,20 +278,29 @@
     tile_count = slots.shape[0]
     row_count = lax.axis_size("row")
     col_count = lax.axis_size("col")
-    scalars = jnp.where(
-        lax.broadcasted_iota(jnp.int32, (8, LANES), 0) == 0, primal_weight, step_start
-    )
     smem = pltpu.SMEM
     halves = width // LANES
 
     def array(*shape):
         return jax.ShapeDtypeStruct(shape, jnp.float32)
 
-    (sent,) = call(
+    sent, scalars = call(
         functools.partial(start_kernel, col_tiles=col_tiles),
-        [array(tile_count * (halves + 1), LANES)],
-        [slots, tile_set, dual_start],
-        spaces={0: smem},
+        [array(tile_count * (halves + 1), LANES), array(8, LANES)],
+        [
+            pltpu.with_memory_space_constraint(slots, pltpu.HBM),
+            pltpu.with_memory_space_constraint(tile_set, pltpu.HBM),
+            pltpu.with_memory_space_constraint(dual_start, pltpu.HBM),
+            primal_weight.reshape(1),
+            step_start.reshape(1),
+        ],
+        scratch=[
+            pltpu.SMEM(slots.shape, jnp.int32),
+            pltpu.VMEM(tile_set.shape, jnp.float32),
+            pltpu.VMEM(dual_start.shape, jnp.float32),
+            pltpu.SemaphoreType.DMA((tile_count + 2,)),
+        ],
+        spaces={0: pltpu.HBM, 1: pltpu.HBM, 2: pltpu.HBM, 3: smem, 4: smem},
     )
     primal, dual = primal_start, dual_start
     hot = step_size = moved = image = None

time: 90.8 us -> 87.5 us (0.964)
  blocking collectives: 32.7 us -> 47.7 us
  starting transfers between devices: 14.9 us -> 7.59 us
  waiting for transfers between devices: 15.1 us -> 8.43 us
  local copies, waits for them, and re-layouts: 6.57 us -> 0.99 us
  Pallas kernels: 19 us -> 20.3 us
    all_to_all x3 -> x4, blocking collectives: 32.7 us -> 47.7 us  [gather_rows(): return lax.all_to_all(copies, 'row', split_axis=0, concat_axis=0)]
    all_to_all x1 -> x0, starting transfers between devices: 7.31 us -> none  [gather_rows(): return lax.all_to_all(copies, 'row', split_axis=0, concat_axis=0)]
    all_to_all x1 -> x0, waiting for transfers between devices: 6.64 us -> none  [gather_rows(): return lax.all_to_all(copies, 'row', split_axis=0, concat_axis=0)]
    unnamed x26 -> x20, local copies, waits for them, and re-layouts: 5.78 us -> 0.94 us
    pallas_call x9, Pallas kernels: 19 us -> 20.3 us  [call(): pl.pallas_call(kernel, out_shape=outs, in_specs=specs, out_specs=[pl.Bloc...]
  transfers between devices with their start and end apart: 13 -> 12, of which waited for: 9 -> 8; matrix products, arithmetic and copies ran while one was open for 0% -> 0% of each run, Pallas kernels for 0% -> 0%
where the time goes in v3:
time: 87.5 us; the launch traced here: 87.2 us
  blocking collectives  47.7 us (55%)
  Pallas kernels  20.3 us (23%)
  waiting for transfers between devices  8.43 us (10%)
  starting transfers between devices  7.59 us (9%)
  between operations  2.19 us (3%)
  local copies, waits for them, and re-layouts  0.99 us (1%)
    all_to_all x4, blocking collectives, gather_rows(): return lax.all_to_all(copies, 'row', split_axis=0, concat_axis=0)  47.7 us
    pallas_call x9, Pallas kernels, call(): pl.pallas_call(kernel, out_shape=outs, in_specs=specs, out_specs=[pl.Bloc...  20.3 us
    ppermute x12, waiting for transfers between devices, exchange(): lax.ppermute(values, axis, [(i, i ^ k) for i in range(size)])  8.43 us
    ppermute x12, starting transfers between devices, exchange(): lax.ppermute(values, axis, [(i, i ^ k) for i in range(size)])  7.59 us
  transfers between devices with their start and end apart: 12, of which 8 were waited for; matrix products, arithmetic and copies ran while one was open for 0% of the time, Pallas kernels for 0%

profile of v3, /device:TPU:0, one launch (start us, length us, event | category | flops | bytes accessed | tf_op | source)
XLA Modules:
  0.0 87.2 jit_solution(6902056312964033106)
XLA Ops:
  0.6 0.0 copy-start.9
  0.6 0.0 copy-start.4
  0.7 0.0 copy-start.3
  0.7 0.0 copy-start.2
  0.7 0.0 copy-start.1
  2.0 0.0 copy-start
  2.0 0.0 copy-start.5
  2.0 0.0 copy-start.6
  2.1 0.0 copy-start.8
  2.1 3.2 %shard_map.131 = (f32[48,128]{1,0:T(8,128)S(1)}, f32[8,128]{1,0:T(8,128)S(1)}) custom-call(s32[16]{0:T(128)} %bitcast.14, f32[16,256,256]{2,1,0:T(8,128)} %bitcast.6, f32[16,256]{1,0:T(8,128)} %refs_6_.6, f32[1]{0:T(128)} %bitcast.4.weight_ref, f32[1]{0:T(128)} %bitcast.5.step_ref), custom_call_target="tpu_custom_call" | custom-call | tf_op jit(solution)/shard_map/pallas_call | solution.py:238
  5.3 15.1 %all_to_all.20.refs_2_ = f32[8,48,128]{2,1,0:T(8,128)S(1)} all-to-all(f32[8,48,128]{2,1,0:T(8,128)S(1)} %broadcast_in_dim.8), channel_id=1, replica_groups=mesh['row'=8,'col'=4] {'row'}, dimensions={0} | all-to-all | bytes 393216 | tf_op jit(solution)/shard_map/all_to_all | solution.py:257
  20.4 0.0 copy-done.9
  20.4 0.0 copy-done.4
  20.4 0.0 copy-done.3
  20.4 0.0 copy-done.2
  20.4 0.0 copy-done.1
  20.4 0.0 copy-done
  20.4 0.0 copy-start.7
  20.4 0.9 %copy-done.7 = f32[128,256]{1,0:T(8,128)S(1)} copy-done((f32[128,256]{1,0:T(8,128)S(1)}, f32[128,256]{1,0:T(8,128)}, u32[]{:S(2)}) %copy-start.7) | copy-done | bytes 131096
  21.3 3.5 %shard_map.132 = (f32[72,128]{1,0:T(8,128)S(1)}, f32[128,256]{1,0:T(8,128)S(1)}, f32[8,128]{1,0:T(8,128)S(1)}, f32[128,128]{1,0:T(8,128)S(1)}) custom-call(s32[16]{0:T(128)S(1)} %bitcast.15, f32[8,128]{1,0:T(8,128)S(1)} %get-tuple-element.29.refs_1_.refs_4_, f32[8,48,128]{2,1,0:T(8,128)S(1)} %all_to_all.20.refs_2_, f32[16,256,256]{2,1,0:T(8,128)S(1)} %bitcast.7, ...), custom_call_target="tpu_custom_call" | custom-call | tf_op jit(solution)/shard_map/pallas_call | solution.py:238
  24.9 0.1 collective-permute-start.2
  24.9 1.6 %collective-permute-start.1 = (f32[72,128]{1,0:T(8,128)S(1)}, f32[72,128]{1,0:T(8,128)S(1)}, u32[]{:S(2)}, u32[]{:S(2)}) collective-permute-start(f32[72,128]{1,0:T(8,128)S(1)} %get-tuple-element.31.refs_0_), channel_id=1, source_target_pairs={{0,2},{1,3},{2,0},{3,1},{4,6},{5,7},{6,4},{7,5},{8,10},{9,11},{10,... | collective-permute-start | bytes 110600 | tf_op jit(solution)/shard_map/ppermute | solution.py:250
  26.5 0.3 collective-permute-start
  26.8 1.9 %collective-permute-done.2.refs_3_ = f32[72,128]{1,0:T(8,128)S(1)} collective-permute-done((f32[72,128]{1,0:T(8,128)S(1)}, f32[72,128]{1,0:T(8,128)S(1)}, u32[]{:S(2)}, u32[]{:S(2)}) %collective-permute-start.2) | collective-permute-done | bytes 36896 | tf_op jit(solution)/shard_map/ppermute | solution.py:250
  28.6 0.4 collective-permute-done.1.refs_2_
  29.1 0.0 collective-permute-done.refs_1_
  29.1 0.0 copy-done.5
  29.1 0.0 copy-done.6
  29.1 0.0 copy-done.8
  29.1 2.0 %shard_map.133 = (f32[16,256]{1,0:T(8,128)S(1)}, f32[40,128]{1,0:T(8,128)S(1)}, f32[16,256]{1,0:T(8,128)S(1)}, f32[8,128]{1,0:T(8,128)S(1)}) custom-call(f32[72,128]{1,0:T(8,128)S(1)} %get-tuple-element.31.refs_0_, f32[72,128]{1,0:T(8,128)S(1)} %collective-permute-done.refs_1_, f32[72,128]{1,0:T(8,128)S(1)} %collective-permute-done.1.refs_2_, ...), custom_call_target="tpu_custom_call" | custom-call | tf_op jit(solution)/shard_map/pallas_call | solution.py:238
  31.1 11.5 %all_to_all.21.refs_2_ = f32[8,40,128]{2,1,0:T(8,128)S(1)} all-to-all(f32[8,40,128]{2,1,0:T(8,128)S(1)} %broadcast_in_dim.9), channel_id=1, replica_groups=mesh['row'=8,'col'=4] {'row'}, dimensions={0} | all-to-all | bytes 327680 | tf_op jit(solution)/shard_map/all_to_all | solution.py:257
  42.6 2.2 %shard_map.134 = (f32[40,128]{1,0:T(8,128)S(1)}, f32[128,256]{1,0:T(8,128)S(1)}, f32[8,128]{1,0:T(8,128)S(1)}) custom-call(s32[16]{0:T(128)S(1)} %bitcast.17, f32[8,128]{1,0:T(8,128)S(1)} %get-tuple-element.29.refs_1_.refs_4_, f32[8,40,128]{2,1,0:T(8,128)S(1)} %all_to_all.21.refs_2_, f32[16,256,256]{2,1,0:T(8,128)S(1)} %bitcast.9, ...), custom_call_target="tpu_custom_call" | custom-call | tf_op jit(solution)/shard_map/pallas_call | solution.py:238
  44.8 0.1 collective-permute-start.5
  44.8 0.9 collective-permute-start.4
  45.7 1.0 %collective-permute-start.3 = (f32[40,128]{1,0:T(8,128)S(1)}, f32[40,128]{1,0:T(8,128)S(1)}, u32[]{:S(2)}, u32[]{:S(2)}) collective-permute-start(f32[40,128]{1,0:T(8,128)S(1)} %get-tuple-element.37.refs_0_), channel_id=1, source_target_pairs={{0,1},{1,0},{2,3},{3,2},{4,5},{5,4},{6,7},{7,6},{8,9},{9,8},{10,11... | collective-permute-start | bytes 61448 | tf_op jit(solution)/shard_map/ppermute | solution.py:250
  46.7 1.3 %collective-permute-done.5.refs_3_ = f32[40,128]{1,0:T(8,128)S(1)} collective-permute-done((f32[40,128]{1,0:T(8,128)S(1)}, f32[40,128]{1,0:T(8,128)S(1)}, u32[]{:S(2)}, u32[]{:S(2)}) %collective-permute-start.5) | collective-permute-done | bytes 20512 | tf_op jit(solution)/shard_map/ppermute | solution.py:250
  48.0 0.7 collective-permute-done.4.refs_2_
  48.7 0.0 collective-permute-done.3.refs_1_
  48.8 2.0 %shard_map.135 = (f32[16,256]{1,0:T(8,128)S(1)}, f32[40,128]{1,0:T(8,128)S(1)}, f32[16,256]{1,0:T(8,128)S(1)}, f32[8,128]{1,0:T(8,128)S(1)}) custom-call(f32[40,128]{1,0:T(8,128)S(1)} %get-tuple-element.37.refs_0_, f32[40,128]{1,0:T(8,128)S(1)} %collective-permute-done.3.refs_1_, f32[40,128]{1,0:T(8,128)S(1)} %collective-permute-done.4.refs_2_, ...), custom_call_target="tpu_custom_call" | custom-call | tf_op jit(solution)/shard_map/pallas_call | solution.py:238
  50.8 10.3 %all_to_all.22.refs_2_ = f32[8,40,128]{2,1,0:T(8,128)S(1)} all-to-all(f32[8,40,128]{2,1,0:T(8,128)S(1)} %broadcast_in_dim.10), channel_id=1, replica_groups=mesh['row'=8,'col'=4] {'row'}, dimensions={0} | all-to-all | bytes 327680 | tf_op jit(solution)/shard_map/all_to_all | solution.py:257
  61.1 2.2 %shard_map.136 = (f32[40,128]{1,0:T(8,128)S(1)}, f32[128,256]{1,0:T(8,128)S(1)}, f32[8,128]{1,0:T(8,128)S(1)}) custom-call(s32[16]{0:T(128)S(1)} %bitcast.19, f32[8,128]{1,0:T(8,128)S(1)} %get-tuple-element.29.refs_1_.refs_4_, f32[8,40,128]{2,1,0:T(8,128)S(1)} %all_to_all.22.refs_2_, f32[16,256,256]{2,1,0:T(8,128)S(1)} %bitcast.11, ...), custom_call_target="tpu_custom_call" | custom-call | tf_op jit(solution)/shard_map/pallas_call | solution.py:238
  63.3 0.1 collective-permute-start.8
  63.3 1.3 %collective-permute-start.7 = (f32[40,128]{1,0:T(8,128)S(1)}, f32[40,128]{1,0:T(8,128)S(1)}, u32[]{:S(2)}, u32[]{:S(2)}) collective-permute-start(f32[40,128]{1,0:T(8,128)S(1)} %get-tuple-element.44.refs_0_), channel_id=1, source_target_pairs={{0,2},{1,3},{2,0},{3,1},{4,6},{5,7},{6,4},{7,5},{8,10},{9,11},{10,... | collective-permute-start | bytes 61448 | tf_op jit(solution)/shard_map/ppermute | solution.py:250
  64.6 0.5 collective-permute-start.6
  65.2 1.4 %collective-permute-done.8.refs_3_ = f32[40,128]{1,0:T(8,128)S(1)} collective-permute-done((f32[40,128]{1,0:T(8,128)S(1)}, f32[40,128]{1,0:T(8,128)S(1)}, u32[]{:S(2)}, u32[]{:S(2)}) %collective-permute-start.8) | collective-permute-done | bytes 20512 | tf_op jit(solution)/shard_map/ppermute | solution.py:250
  66.6 0.6 collective-permute-done.7.refs_2_
  67.2 0.0 collective-permute-done.6.refs_1_
  67.2 2.0 %shard_map.137 = (f32[16,256]{1,0:T(8,128)S(1)}, f32[40,128]{1,0:T(8,128)S(1)}, f32[16,256]{1,0:T(8,128)S(1)}, f32[8,128]{1,0:T(8,128)S(1)}) custom-call(f32[40,128]{1,0:T(8,128)S(1)} %get-tuple-element.44.refs_0_, f32[40,128]{1,0:T(8,128)S(1)} %collective-permute-done.6.refs_1_, f32[40,128]{1,0:T(8,128)S(1)} %collective-permute-done.7.refs_2_, ...), custom_call_target="tpu_custom_call" | custom-call | tf_op jit(solution)/shard_map/pallas_call | solution.py:238
  69.2 10.9 %all_to_all.23.refs_2_ = f32[8,40,128]{2,1,0:T(8,128)S(1)} all-to-all(f32[8,40,128]{2,1,0:T(8,128)S(1)} %broadcast_in_dim.11), channel_id=1, replica_groups=mesh['row'=8,'col'=4] {'row'}, dimensions={0} | all-to-all | bytes 327680 | tf_op jit(solution)/shard_map/all_to_all | solution.py:257
  80.1 2.6 %shard_map.138 = (f32[40,128]{1,0:T(8,128)S(1)}, f32[128,256]{1,0:T(8,128)}, f32[8,128]{1,0:T(8,128)S(1)}) custom-call(s32[16]{0:T(128)S(1)} %bitcast.21, f32[8,128]{1,0:T(8,128)S(1)} %get-tuple-element.29.refs_1_.refs_4_, f32[8,40,128]{2,1,0:T(8,128)S(1)} %all_to_all.23.refs_2_, f32[16,256,256]{2,1,0:T(8,128)S(1)} %bitcast.13, ...), custom_call_target="tpu_custom_call" | custom-call | tf_op jit(solution)/shard_map/pallas_call | solution.py:238
  82.7 0.0 collective-permute-start.11
  82.7 0.8 collective-permute-start.10
  83.4 1.1 %collective-permute-start.9 = (f32[40,128]{1,0:T(8,128)S(1)}, f32[40,128]{1,0:T(8,128)S(1)}, u32[]{:S(2)}, u32[]{:S(2)}) collective-permute-start(f32[40,128]{1,0:T(8,128)S(1)} %get-tuple-element.52.refs_0_), channel_id=1, source_target_pairs={{0,1},{1,0},{2,3},{3,2},{4,5},{5,4},{6,7},{7,6},{8,9},{9,8},{10,11... | collective-permute-start | bytes 61448 | tf_op jit(solution)/shard_map/ppermute | solution.py:250
  84.6 1.3 %collective-permute-done.11.refs_3_ = f32[40,128]{1,0:T(8,128)S(1)} collective-permute-done((f32[40,128]{1,0:T(8,128)S(1)}, f32[40,128]{1,0:T(8,128)S(1)}, u32[]{:S(2)}, u32[]{:S(2)}) %collective-permute-start.11) | collective-permute-done | bytes 20512 | tf_op jit(solution)/shard_map/ppermute | solution.py:250
  85.9 0.7 collective-permute-done.10.refs_2_
  86.6 0.0 collective-permute-done.9.refs_1_
  86.6 0.6 shard_map.139
  (4 shorter events, 0.1 us)
Async XLA Ops:
  0.6 19.7 %copy-start.9 = (s32[1,1,16]{2,1,0:T(1,128)S(1)}, s32[1,1,16]{2,1,0:T(1,128)}, u32[]{:S(2)}) copy-start(s32[1,1,16]{2,1,0:T(1,128)} %param.13) | copy-start | bytes 196
  0.6 19.7 %copy-start.4 = (s32[128,256]{1,0:T(8,128)S(1)}, s32[128,256]{1,0:T(8,128)}, u32[]{:S(2)}) copy-start(s32[128,256]{1,0:T(8,128)} %refs_8_.14) | copy-start | bytes 393220
  0.7 19.7 %copy-start.3 = (f32[128,256]{1,0:T(8,128)S(1)}, f32[128,256]{1,0:T(8,128)}, u32[]{:S(2)}) copy-start(f32[128,256]{1,0:T(8,128)} %refs_7_.14) | copy-start | bytes 393220
  0.7 19.7 %copy-start.2 = (f32[128,256]{1,0:T(8,128)S(1)}, f32[128,256]{1,0:T(8,128)}, u32[]{:S(2)}) copy-start(f32[128,256]{1,0:T(8,128)} %refs_6_.9) | copy-start | bytes 393220
  0.7 19.7 %copy-start.1 = (f32[128,256]{1,0:T(8,128)S(1)}, f32[128,256]{1,0:T(8,128)}, u32[]{:S(2)}) copy-start(f32[128,256]{1,0:T(8,128)} %refs_5_.7) | copy-start | bytes 393220
  2.0 18.4 %copy-start = (f32[1,1,16,256,256]{4,3,2,1,0:T(8,128)S(1)}, f32[1,1,16,256,256]{4,3,2,1,0:T(8,128)}, u32[]{:S(2)}) copy-start(f32[1,1,16,256,256]{4,3,2,1,0:T(8,128)} %param.12) | copy-start | bytes 12582916
  2.0 27.0 %copy-start.5 = (f32[16,256]{1,0:T(8,128)S(1)}, f32[16,256]{1,0:T(8,128)}, u32[]{:S(2)}) copy-start(f32[16,256]{1,0:T(8,128)} %refs_7_.15) | copy-start | bytes 49156
  2.0 27.0 %copy-start.6 = (s32[16,256]{1,0:T(8,128)S(1)}, s32[16,256]{1,0:T(8,128)}, u32[]{:S(2)}) copy-start(s32[16,256]{1,0:T(8,128)} %refs_8_.15) | copy-start | bytes 49156
  2.1 27.0 %copy-start.8 = (f32[16,256]{1,0:T(8,128)S(1)}, f32[16,256]{1,0:T(8,128)}, u32[]{:S(2)}) copy-start(f32[16,256]{1,0:T(8,128)} %refs_6_.6) | copy-start | bytes 49156
  20.4 0.9 %copy-start.7 = (f32[128,256]{1,0:T(8,128)S(1)}, f32[128,256]{1,0:T(8,128)}, u32[]{:S(2)}) copy-start(f32[128,256]{1,0:T(8,128)} %refs_4_.1) | copy-start | bytes 393220
  24.9 3.8 %collective-permute-start.2 = (f32[72,128]{1,0:T(8,128)S(1)}, f32[72,128]{1,0:T(8,128)S(1)}, u32[]{:S(2)}, u32[]{:S(2)}) collective-permute-start(f32[72,128]{1,0:T(8,128)S(1)} %get-tuple-element.31.refs_0_), channel_id=1, source_target_pairs={{0,3},{1,2},{2,1},{3,0},{4,7},{5,6},{6,5},{7,4},{8,11},{9,10},{10,... | collective-permute-start | bytes 110600 | tf_op jit(solution)/shard_map/ppermute | solution.py:250
  24.9 4.2 %collective-permute-start.1 = (f32[72,128]{1,0:T(8,128)S(1)}, f32[72,128]{1,0:T(8,128)S(1)}, u32[]{:S(2)}, u32[]{:S(2)}) collective-permute-start(f32[72,128]{1,0:T(8,128)S(1)} %get-tuple-element.31.refs_0_), channel_id=1, source_target_pairs={{0,2},{1,3},{2,0},{3,1},{4,6},{5,7},{6,4},{7,5},{8,10},{9,11},{10,... | collective-permute-start | bytes 110600 | tf_op jit(solution)/shard_map/ppermute | solution.py:250
  26.5 2.6 %collective-permute-start = (f32[72,128]{1,0:T(8,128)S(1)}, f32[72,128]{1,0:T(8,128)S(1)}, u32[]{:S(2)}, u32[]{:S(2)}) collective-permute-start(f32[72,128]{1,0:T(8,128)S(1)} %get-tuple-element.31.refs_0_), channel_id=1, source_target_pairs={{0,1},{1,0},{2,3},{3,2},{4,5},{5,4},{6,7},{7,6},{8,9},{9,8},{10,11... | collective-permute-start | bytes 110600 | tf_op jit(solution)/shard_map/ppermute | solution.py:250
  44.8 3.3 %collective-permute-start.5 = (f32[40,128]{1,0:T(8,128)S(1)}, f32[40,128]{1,0:T(8,128)S(1)}, u32[]{:S(2)}, u32[]{:S(2)}) collective-permute-start(f32[40,128]{1,0:T(8,128)S(1)} %get-tuple-element.37.refs_0_), channel_id=1, source_target_pairs={{0,3},{1,2},{2,1},{3,0},{4,7},{5,6},{6,5},{7,4},{8,11},{9,10},{10,... | collective-permute-start | bytes 61448 | tf_op jit(solution)/shard_map/ppermute | solution.py:250
  44.8 3.9 %collective-permute-start.4 = (f32[40,128]{1,0:T(8,128)S(1)}, f32[40,128]{1,0:T(8,128)S(1)}, u32[]{:S(2)}, u32[]{:S(2)}) collective-permute-start(f32[40,128]{1,0:T(8,128)S(1)} %get-tuple-element.37.refs_0_), channel_id=1, source_target_pairs={{0,2},{1,3},{2,0},{3,1},{4,6},{5,7},{6,4},{7,5},{8,10},{9,11},{10,... | collective-permute-start | bytes 61448 | tf_op jit(solution)/shard_map/ppermute | solution.py:250
  45.7 3.1 %collective-permute-start.3 = (f32[40,128]{1,0:T(8,128)S(1)}, f32[40,128]{1,0:T(8,128)S(1)}, u32[]{:S(2)}, u32[]{:S(2)}) collective-permute-start(f32[40,128]{1,0:T(8,128)S(1)} %get-tuple-element.37.refs_0_), channel_id=1, source_target_pairs={{0,1},{1,0},{2,3},{3,2},{4,5},{5,4},{6,7},{7,6},{8,9},{9,8},{10,11... | collective-permute-start | bytes 61448 | tf_op jit(solution)/shard_map/ppermute | solution.py:250
  63.3 3.3 %collective-permute-start.8 = (f32[40,128]{1,0:T(8,128)S(1)}, f32[40,128]{1,0:T(8,128)S(1)}, u32[]{:S(2)}, u32[]{:S(2)}) collective-permute-start(f32[40,128]{1,0:T(8,128)S(1)} %get-tuple-element.44.refs_0_), channel_id=1, source_target_pairs={{0,3},{1,2},{2,1},{3,0},{4,7},{5,6},{6,5},{7,4},{8,11},{9,10},{10,... | collective-permute-start | bytes 61448 | tf_op jit(solution)/shard_map/ppermute | solution.py:250
  63.3 3.8 %collective-permute-start.7 = (f32[40,128]{1,0:T(8,128)S(1)}, f32[40,128]{1,0:T(8,128)S(1)}, u32[]{:S(2)}, u32[]{:S(2)}) collective-permute-start(f32[40,128]{1,0:T(8,128)S(1)} %get-tuple-element.44.refs_0_), channel_id=1, source_target_pairs={{0,2},{1,3},{2,0},{3,1},{4,6},{5,7},{6,4},{7,5},{8,10},{9,11},{10,... | collective-permute-start | bytes 61448 | tf_op jit(solution)/shard_map/ppermute | solution.py:250
  64.6 2.5 %collective-permute-start.6 = (f32[40,128]{1,0:T(8,128)S(1)}, f32[40,128]{1,0:T(8,128)S(1)}, u32[]{:S(2)}, u32[]{:S(2)}) collective-permute-start(f32[40,128]{1,0:T(8,128)S(1)} %get-tuple-element.44.refs_0_), channel_id=1, source_target_pairs={{0,1},{1,0},{2,3},{3,2},{4,5},{5,4},{6,7},{7,6},{8,9},{9,8},{10,11... | collective-permute-start | bytes 61448 | tf_op jit(solution)/shard_map/ppermute | solution.py:250
  82.7 3.2 %collective-permute-start.11 = (f32[40,128]{1,0:T(8,128)S(1)}, f32[40,128]{1,0:T(8,128)S(1)}, u32[]{:S(2)}, u32[]{:S(2)}) collective-permute-start(f32[40,128]{1,0:T(8,128)S(1)} %get-tuple-element.52.refs_0_), channel_id=1, source_target_pairs={{0,3},{1,2},{2,1},{3,0},{4,7},{5,6},{6,5},{7,4},{8,11},{9,10},{10,... | collective-permute-start | bytes 61448 | tf_op jit(solution)/shard_map/ppermute | solution.py:250
  82.7 3.9 %collective-permute-start.10 = (f32[40,128]{1,0:T(8,128)S(1)}, f32[40,128]{1,0:T(8,128)S(1)}, u32[]{:S(2)}, u32[]{:S(2)}) collective-permute-start(f32[40,128]{1,0:T(8,128)S(1)} %get-tuple-element.52.refs_0_), channel_id=1, source_target_pairs={{0,2},{1,3},{2,0},{3,1},{4,6},{5,7},{6,4},{7,5},{8,10},{9,11},{10,... | collective-permute-start | bytes 61448 | tf_op jit(solution)/shard_map/ppermute | solution.py:250
  83.4 3.1 %collective-permute-start.9 = (f32[40,128]{1,0:T(8,128)S(1)}, f32[40,128]{1,0:T(8,128)S(1)}, u32[]{:S(2)}, u32[]{:S(2)}) collective-permute-start(f32[40,128]{1,0:T(8,128)S(1)} %get-tuple-element.52.refs_0_), channel_id=1, source_target_pairs={{0,1},{1,0},{2,3},{3,2},{4,5},{5,4},{6,7},{7,6},{8,9},{9,8},{10,11... | collective-permute-start | bytes 61448 | tf_op jit(solution)/shard_map/ppermute | solution.py:250

commit v4 on v3

--- a/solution.py
+++ b/solution.py
@@ -33,7 +33,7 @@
         product = jnp.sum(tiles_ref[t] * picked, axis=1, keepdims=True)
         return total + jnp.where(lane == slot // col_tiles, product, 0.0)
 
-    total = lax.fori_loop(0, tile_count, step, jnp.zeros((height, 128), jnp.float32), unroll=2)
+    total = lax.fori_loop(0, tile_count, step, jnp.zeros((height, 128), jnp.float32), unroll=4)
     return total.T[:row_tiles]
 
 
@@ -54,7 +54,7 @@
             out_ref[pl.ds(h * tile_count + t, 1), :] = product[:, h * LANES : (h + 1) * LANES]
         return carry
 
-    lax.fori_loop(0, tile_count, step, 0, unroll=2)
+    lax.fori_loop(0, tile_count, step, 0, unroll=4)
 
 
 def pack(out_ref, values, start=0):

time: 87.5 us -> 84.9 us (0.970)
  Pallas kernels: 20.3 us -> 17.7 us
    pallas_call x9, Pallas kernels: 20.3 us -> 17.7 us  [call(): pl.pallas_call(kernel, out_shape=outs, in_specs=specs, out_specs=[pl.Bloc...]
where the time goes in v4:
time: 84.9 us; the launch traced here: 84.6 us
  blocking collectives  47.7 us (56%)
  Pallas kernels  17.7 us (21%)
  waiting for transfers between devices  8.43 us (10%)
  starting transfers between devices  7.59 us (9%)
  between operations  2.2 us (3%)
  local copies, waits for them, and re-layouts  0.99 us (1%)
    all_to_all x4, blocking collectives, gather_rows(): return lax.all_to_all(copies, 'row', split_axis=0, concat_axis=0)  47.7 us
    pallas_call x9, Pallas kernels, call(): pl.pallas_call(kernel, out_shape=outs, in_specs=specs, out_specs=[pl.Bloc...  17.7 us
    ppermute x12, waiting for transfers between devices, exchange(): lax.ppermute(values, axis, [(i, i ^ k) for i in range(size)])  8.43 us
    ppermute x12, starting transfers between devices, exchange(): lax.ppermute(values, axis, [(i, i ^ k) for i in range(size)])  7.59 us
  transfers between devices with their start and end apart: 12, of which 8 were waited for; matrix products, arithmetic and copies ran while one was open for 0% of the time, Pallas kernels for 0%

profile of v4, /device:TPU:0, one launch (start us, length us, event | category | flops | bytes accessed | tf_op | source)
XLA Modules:
  0.0 84.6 jit_solution(6377253677588013498)
XLA Ops:
  0.6 0.0 copy-start.9
  0.6 0.0 copy-start.4
  0.7 0.0 copy-start.3
  0.7 0.0 copy-start.2
  0.7 0.0 copy-start.1
  2.0 0.0 copy-start
  2.0 0.0 copy-start.5
  2.0 0.0 copy-start.6
  2.1 0.0 copy-start.8
  2.1 3.2 %shard_map.131 = (f32[48,128]{1,0:T(8,128)S(1)}, f32[8,128]{1,0:T(8,128)S(1)}) custom-call(s32[16]{0:T(128)} %bitcast.14, f32[16,256,256]{2,1,0:T(8,128)} %bitcast.6, f32[16,256]{1,0:T(8,128)} %refs_6_.6, f32[1]{0:T(128)} %bitcast.4.weight_ref, f32[1]{0:T(128)} %bitcast.5.step_ref), custom_call_target="tpu_custom_call" | custom-call | tf_op jit(solution)/shard_map/pallas_call | solution.py:238
  5.3 15.1 %all_to_all.20.refs_2_ = f32[8,48,128]{2,1,0:T(8,128)S(1)} all-to-all(f32[8,48,128]{2,1,0:T(8,128)S(1)} %broadcast_in_dim.8), channel_id=1, replica_groups=mesh['row'=8,'col'=4] {'row'}, dimensions={0} | all-to-all | bytes 393216 | tf_op jit(solution)/shard_map/all_to_all | solution.py:257
  20.4 0.0 copy-done.9
  20.4 0.0 copy-done.4
  20.4 0.0 copy-done.3
  20.4 0.0 copy-done.2
  20.4 0.0 copy-done.1
  20.4 0.0 copy-done
  20.4 0.0 copy-start.7
  20.4 0.9 %copy-done.7 = f32[128,256]{1,0:T(8,128)S(1)} copy-done((f32[128,256]{1,0:T(8,128)S(1)}, f32[128,256]{1,0:T(8,128)}, u32[]{:S(2)}) %copy-start.7) | copy-done | bytes 131096
  21.3 2.9 %shard_map.132 = (f32[72,128]{1,0:T(8,128)S(1)}, f32[128,256]{1,0:T(8,128)S(1)}, f32[8,128]{1,0:T(8,128)S(1)}, f32[128,128]{1,0:T(8,128)S(1)}) custom-call(s32[16]{0:T(128)S(1)} %bitcast.15, f32[8,128]{1,0:T(8,128)S(1)} %get-tuple-element.29.refs_1_.refs_4_, f32[8,48,128]{2,1,0:T(8,128)S(1)} %all_to_all.20.refs_2_, f32[16,256,256]{2,1,0:T(8,128)S(1)} %bitcast.7, ...), custom_call_target="tpu_custom_call" | custom-call | tf_op jit(solution)/shard_map/pallas_call | solution.py:238
  24.2 0.1 collective-permute-start.2
  24.3 1.6 %collective-permute-start.1 = (f32[72,128]{1,0:T(8,128)S(1)}, f32[72,128]{1,0:T(8,128)S(1)}, u32[]{:S(2)}, u32[]{:S(2)}) collective-permute-start(f32[72,128]{1,0:T(8,128)S(1)} %get-tuple-element.31.refs_0_), channel_id=1, source_target_pairs={{0,2},{1,3},{2,0},{3,1},{4,6},{5,7},{6,4},{7,5},{8,10},{9,11},{10,... | collective-permute-start | bytes 110600 | tf_op jit(solution)/shard_map/ppermute | solution.py:250
  25.8 0.3 collective-permute-start
  26.1 1.9 %collective-permute-done.2.refs_3_ = f32[72,128]{1,0:T(8,128)S(1)} collective-permute-done((f32[72,128]{1,0:T(8,128)S(1)}, f32[72,128]{1,0:T(8,128)S(1)}, u32[]{:S(2)}, u32[]{:S(2)}) %collective-permute-start.2) | collective-permute-done | bytes 36896 | tf_op jit(solution)/shard_map/ppermute | solution.py:250
  28.0 0.4 collective-permute-done.1.refs_2_
  28.4 0.0 collective-permute-done.refs_1_
  28.4 0.0 copy-done.5
  28.4 0.0 copy-done.6
  28.5 0.0 copy-done.8
  28.5 1.6 %shard_map.133 = (f32[16,256]{1,0:T(8,128)S(1)}, f32[40,128]{1,0:T(8,128)S(1)}, f32[16,256]{1,0:T(8,128)S(1)}, f32[8,128]{1,0:T(8,128)S(1)}) custom-call(f32[72,128]{1,0:T(8,128)S(1)} %get-tuple-element.31.refs_0_, f32[72,128]{1,0:T(8,128)S(1)} %collective-permute-done.refs_1_, f32[72,128]{1,0:T(8,128)S(1)} %collective-permute-done.1.refs_2_, ...), custom_call_target="tpu_custom_call" | custom-call | tf_op jit(solution)/shard_map/pallas_call | solution.py:238
  30.1 11.5 %all_to_all.21.refs_2_ = f32[8,40,128]{2,1,0:T(8,128)S(1)} all-to-all(f32[8,40,128]{2,1,0:T(8,128)S(1)} %broadcast_in_dim.9), channel_id=1, replica_groups=mesh['row'=8,'col'=4] {'row'}, dimensions={0} | all-to-all | bytes 327680 | tf_op jit(solution)/shard_map/all_to_all | solution.py:257
  41.6 1.9 %shard_map.134 = (f32[40,128]{1,0:T(8,128)S(1)}, f32[128,256]{1,0:T(8,128)S(1)}, f32[8,128]{1,0:T(8,128)S(1)}) custom-call(s32[16]{0:T(128)S(1)} %bitcast.17, f32[8,128]{1,0:T(8,128)S(1)} %get-tuple-element.29.refs_1_.refs_4_, f32[8,40,128]{2,1,0:T(8,128)S(1)} %all_to_all.21.refs_2_, f32[16,256,256]{2,1,0:T(8,128)S(1)} %bitcast.9, ...), custom_call_target="tpu_custom_call" | custom-call | tf_op jit(solution)/shard_map/pallas_call | solution.py:238
  43.4 0.1 collective-permute-start.5
  43.5 0.8 %collective-permute-start.4 = (f32[40,128]{1,0:T(8,128)S(1)}, f32[40,128]{1,0:T(8,128)S(1)}, u32[]{:S(2)}, u32[]{:S(2)}) collective-permute-start(f32[40,128]{1,0:T(8,128)S(1)} %get-tuple-element.37.refs_0_), channel_id=1, source_target_pairs={{0,2},{1,3},{2,0},{3,1},{4,6},{5,7},{6,4},{7,5},{8,10},{9,11},{10,... | collective-permute-start | bytes 61448 | tf_op jit(solution)/shard_map/ppermute | solution.py:250
  44.4 1.0 %collective-permute-start.3 = (f32[40,128]{1,0:T(8,128)S(1)}, f32[40,128]{1,0:T(8,128)S(1)}, u32[]{:S(2)}, u32[]{:S(2)}) collective-permute-start(f32[40,128]{1,0:T(8,128)S(1)} %get-tuple-element.37.refs_0_), channel_id=1, source_target_pairs={{0,1},{1,0},{2,3},{3,2},{4,5},{5,4},{6,7},{7,6},{8,9},{9,8},{10,11... | collective-permute-start | bytes 61448 | tf_op jit(solution)/shard_map/ppermute | solution.py:250
  45.4 1.3 %collective-permute-done.5.refs_3_ = f32[40,128]{1,0:T(8,128)S(1)} collective-permute-done((f32[40,128]{1,0:T(8,128)S(1)}, f32[40,128]{1,0:T(8,128)S(1)}, u32[]{:S(2)}, u32[]{:S(2)}) %collective-permute-start.5) | collective-permute-done | bytes 20512 | tf_op jit(solution)/shard_map/ppermute | solution.py:250
  46.7 0.7 collective-permute-done.4.refs_2_
  47.4 0.0 collective-permute-done.3.refs_1_
  47.4 1.6 %shard_map.135 = (f32[16,256]{1,0:T(8,128)S(1)}, f32[40,128]{1,0:T(8,128)S(1)}, f32[16,256]{1,0:T(8,128)S(1)}, f32[8,128]{1,0:T(8,128)S(1)}) custom-call(f32[40,128]{1,0:T(8,128)S(1)} %get-tuple-element.37.refs_0_, f32[40,128]{1,0:T(8,128)S(1)} %collective-permute-done.3.refs_1_, f32[40,128]{1,0:T(8,128)S(1)} %collective-permute-done.4.refs_2_, ...), custom_call_target="tpu_custom_call" | custom-call | tf_op jit(solution)/shard_map/pallas_call | solution.py:238
  49.1 10.3 %all_to_all.22.refs_2_ = f32[8,40,128]{2,1,0:T(8,128)S(1)} all-to-all(f32[8,40,128]{2,1,0:T(8,128)S(1)} %broadcast_in_dim.10), channel_id=1, replica_groups=mesh['row'=8,'col'=4] {'row'}, dimensions={0} | all-to-all | bytes 327680 | tf_op jit(solution)/shard_map/all_to_all | solution.py:257
  59.4 1.9 %shard_map.136 = (f32[40,128]{1,0:T(8,128)S(1)}, f32[128,256]{1,0:T(8,128)S(1)}, f32[8,128]{1,0:T(8,128)S(1)}) custom-call(s32[16]{0:T(128)S(1)} %bitcast.19, f32[8,128]{1,0:T(8,128)S(1)} %get-tuple-element.29.refs_1_.refs_4_, f32[8,40,128]{2,1,0:T(8,128)S(1)} %all_to_all.22.refs_2_, f32[16,256,256]{2,1,0:T(8,128)S(1)} %bitcast.11, ...), custom_call_target="tpu_custom_call" | custom-call | tf_op jit(solution)/shard_map/pallas_call | solution.py:238
  61.3 0.1 collective-permute-start.8
  61.3 1.3 %collective-permute-start.7 = (f32[40,128]{1,0:T(8,128)S(1)}, f32[40,128]{1,0:T(8,128)S(1)}, u32[]{:S(2)}, u32[]{:S(2)}) collective-permute-start(f32[40,128]{1,0:T(8,128)S(1)} %get-tuple-element.44.refs_0_), channel_id=1, source_target_pairs={{0,2},{1,3},{2,0},{3,1},{4,6},{5,7},{6,4},{7,5},{8,10},{9,11},{10,... | collective-permute-start | bytes 61448 | tf_op jit(solution)/shard_map/ppermute | solution.py:250
  62.6 0.5 collective-permute-start.6
  63.2 1.4 %collective-permute-done.8.refs_3_ = f32[40,128]{1,0:T(8,128)S(1)} collective-permute-done((f32[40,128]{1,0:T(8,128)S(1)}, f32[40,128]{1,0:T(8,128)S(1)}, u32[]{:S(2)}, u32[]{:S(2)}) %collective-permute-start.8) | collective-permute-done | bytes 20512 | tf_op jit(solution)/shard_map/ppermute | solution.py:250
  64.5 0.6 collective-permute-done.7.refs_2_
  65.2 0.0 collective-permute-done.6.refs_1_
  65.2 1.6 %shard_map.137 = (f32[16,256]{1,0:T(8,128)S(1)}, f32[40,128]{1,0:T(8,128)S(1)}, f32[16,256]{1,0:T(8,128)S(1)}, f32[8,128]{1,0:T(8,128)S(1)}) custom-call(f32[40,128]{1,0:T(8,128)S(1)} %get-tuple-element.44.refs_0_, f32[40,128]{1,0:T(8,128)S(1)} %collective-permute-done.6.refs_1_, f32[40,128]{1,0:T(8,128)S(1)} %collective-permute-done.7.refs_2_, ...), custom_call_target="tpu_custom_call" | custom-call | tf_op jit(solution)/shard_map/pallas_call | solution.py:238
  66.8 10.9 %all_to_all.23.refs_2_ = f32[8,40,128]{2,1,0:T(8,128)S(1)} all-to-all(f32[8,40,128]{2,1,0:T(8,128)S(1)} %broadcast_in_dim.11), channel_id=1, replica_groups=mesh['row'=8,'col'=4] {'row'}, dimensions={0} | all-to-all | bytes 327680 | tf_op jit(solution)/shard_map/all_to_all | solution.py:257
  77.7 2.4 %shard_map.138 = (f32[40,128]{1,0:T(8,128)S(1)}, f32[128,256]{1,0:T(8,128)}, f32[8,128]{1,0:T(8,128)S(1)}) custom-call(s32[16]{0:T(128)S(1)} %bitcast.21, f32[8,128]{1,0:T(8,128)S(1)} %get-tuple-element.29.refs_1_.refs_4_, f32[8,40,128]{2,1,0:T(8,128)S(1)} %all_to_all.23.refs_2_, f32[16,256,256]{2,1,0:T(8,128)S(1)} %bitcast.13, ...), custom_call_target="tpu_custom_call" | custom-call | tf_op jit(solution)/shard_map/pallas_call | solution.py:238
  80.0 0.0 collective-permute-start.11
  80.0 0.8 collective-permute-start.10
  80.8 1.1 %collective-permute-start.9 = (f32[40,128]{1,0:T(8,128)S(1)}, f32[40,128]{1,0:T(8,128)S(1)}, u32[]{:S(2)}, u32[]{:S(2)}) collective-permute-start(f32[40,128]{1,0:T(8,128)S(1)} %get-tuple-element.52.refs_0_), channel_id=1, source_target_pairs={{0,1},{1,0},{2,3},{3,2},{4,5},{5,4},{6,7},{7,6},{8,9},{9,8},{10,11... | collective-permute-start | bytes 61448 | tf_op jit(solution)/shard_map/ppermute | solution.py:250
  81.9 1.3 %collective-permute-done.11.refs_3_ = f32[40,128]{1,0:T(8,128)S(1)} collective-permute-done((f32[40,128]{1,0:T(8,128)S(1)}, f32[40,128]{1,0:T(8,128)S(1)}, u32[]{:S(2)}, u32[]{:S(2)}) %collective-permute-start.11) | collective-permute-done | bytes 20512 | tf_op jit(solution)/shard_map/ppermute | solution.py:250
  83.3 0.7 collective-permute-done.10.refs_2_
  83.9 0.0 collective-permute-done.9.refs_1_
  84.0 0.6 shard_map.139
  (4 shorter events, 0.1 us)
Async XLA Ops:
  0.6 19.7 %copy-start.9 = (s32[1,1,16]{2,1,0:T(1,128)S(1)}, s32[1,1,16]{2,1,0:T(1,128)}, u32[]{:S(2)}) copy-start(s32[1,1,16]{2,1,0:T(1,128)} %param.13) | copy-start | bytes 196
  0.6 19.7 %copy-start.4 = (s32[128,256]{1,0:T(8,128)S(1)}, s32[128,256]{1,0:T(8,128)}, u32[]{:S(2)}) copy-start(s32[128,256]{1,0:T(8,128)} %refs_8_.14) | copy-start | bytes 393220
  0.7 19.7 %copy-start.3 = (f32[128,256]{1,0:T(8,128)S(1)}, f32[128,256]{1,0:T(8,128)}, u32[]{:S(2)}) copy-start(f32[128,256]{1,0:T(8,128)} %refs_7_.14) | copy-start | bytes 393220
  0.7 19.7 %copy-start.2 = (f32[128,256]{1,0:T(8,128)S(1)}, f32[128,256]{1,0:T(8,128)}, u32[]{:S(2)}) copy-start(f32[128,256]{1,0:T(8,128)} %refs_6_.9) | copy-start | bytes 393220
  0.7 19.7 %copy-start.1 = (f32[128,256]{1,0:T(8,128)S(1)}, f32[128,256]{1,0:T(8,128)}, u32[]{:S(2)}) copy-start(f32[128,256]{1,0:T(8,128)} %refs_5_.7) | copy-start | bytes 393220
  2.0 18.4 %copy-start = (f32[1,1,16,256,256]{4,3,2,1,0:T(8,128)S(1)}, f32[1,1,16,256,256]{4,3,2,1,0:T(8,128)}, u32[]{:S(2)}) copy-start(f32[1,1,16,256,256]{4,3,2,1,0:T(8,128)} %param.12) | copy-start | bytes 12582916
  2.0 26.4 %copy-start.5 = (f32[16,256]{1,0:T(8,128)S(1)}, f32[16,256]{1,0:T(8,128)}, u32[]{:S(2)}) copy-start(f32[16,256]{1,0:T(8,128)} %refs_7_.15) | copy-start | bytes 49156
  2.0 26.4 %copy-start.6 = (s32[16,256]{1,0:T(8,128)S(1)}, s32[16,256]{1,0:T(8,128)}, u32[]{:S(2)}) copy-start(s32[16,256]{1,0:T(8,128)} %refs_8_.15) | copy-start | bytes 49156
  2.1 26.4 %copy-start.8 = (f32[16,256]{1,0:T(8,128)S(1)}, f32[16,256]{1,0:T(8,128)}, u32[]{:S(2)}) copy-start(f32[16,256]{1,0:T(8,128)} %refs_6_.6) | copy-start | bytes 49156
  20.4 0.9 %copy-start.7 = (f32[128,256]{1,0:T(8,128)S(1)}, f32[128,256]{1,0:T(8,128)}, u32[]{:S(2)}) copy-start(f32[128,256]{1,0:T(8,128)} %refs_4_.1) | copy-start | bytes 393220
  24.2 3.8 %collective-permute-start.2 = (f32[72,128]{1,0:T(8,128)S(1)}, f32[72,128]{1,0:T(8,128)S(1)}, u32[]{:S(2)}, u32[]{:S(2)}) collective-permute-start(f32[72,128]{1,0:T(8,128)S(1)} %get-tuple-element.31.refs_0_), channel_id=1, source_target_pairs={{0,3},{1,2},{2,1},{3,0},{4,7},{5,6},{6,5},{7,4},{8,11},{9,10},{10,... | collective-permute-start | bytes 110600 | tf_op jit(solution)/shard_map/ppermute | solution.py:250
  24.3 4.2 %collective-permute-start.1 = (f32[72,128]{1,0:T(8,128)S(1)}, f32[72,128]{1,0:T(8,128)S(1)}, u32[]{:S(2)}, u32[]{:S(2)}) collective-permute-start(f32[72,128]{1,0:T(8,128)S(1)} %get-tuple-element.31.refs_0_), channel_id=1, source_target_pairs={{0,2},{1,3},{2,0},{3,1},{4,6},{5,7},{6,4},{7,5},{8,10},{9,11},{10,... | collective-permute-start | bytes 110600 | tf_op jit(solution)/shard_map/ppermute | solution.py:250
  25.8 2.6 %collective-permute-start = (f32[72,128]{1,0:T(8,128)S(1)}, f32[72,128]{1,0:T(8,128)S(1)}, u32[]{:S(2)}, u32[]{:S(2)}) collective-permute-start(f32[72,128]{1,0:T(8,128)S(1)} %get-tuple-element.31.refs_0_), channel_id=1, source_target_pairs={{0,1},{1,0},{2,3},{3,2},{4,5},{5,4},{6,7},{7,6},{8,9},{9,8},{10,11... | collective-permute-start | bytes 110600 | tf_op jit(solution)/shard_map/ppermute | solution.py:250
  43.4 3.3 %collective-permute-start.5 = (f32[40,128]{1,0:T(8,128)S(1)}, f32[40,128]{1,0:T(8,128)S(1)}, u32[]{:S(2)}, u32[]{:S(2)}) collective-permute-start(f32[40,128]{1,0:T(8,128)S(1)} %get-tuple-element.37.refs_0_), channel_id=1, source_target_pairs={{0,3},{1,2},{2,1},{3,0},{4,7},{5,6},{6,5},{7,4},{8,11},{9,10},{10,... | collective-permute-start | bytes 61448 | tf_op jit(solution)/shard_map/ppermute | solution.py:250
  43.5 3.9 %collective-permute-start.4 = (f32[40,128]{1,0:T(8,128)S(1)}, f32[40,128]{1,0:T(8,128)S(1)}, u32[]{:S(2)}, u32[]{:S(2)}) collective-permute-start(f32[40,128]{1,0:T(8,128)S(1)} %get-tuple-element.37.refs_0_), channel_id=1, source_target_pairs={{0,2},{1,3},{2,0},{3,1},{4,6},{5,7},{6,4},{7,5},{8,10},{9,11},{10,... | collective-permute-start | bytes 61448 | tf_op jit(solution)/shard_map/ppermute | solution.py:250
  44.4 3.1 %collective-permute-start.3 = (f32[40,128]{1,0:T(8,128)S(1)}, f32[40,128]{1,0:T(8,128)S(1)}, u32[]{:S(2)}, u32[]{:S(2)}) collective-permute-start(f32[40,128]{1,0:T(8,128)S(1)} %get-tuple-element.37.refs_0_), channel_id=1, source_target_pairs={{0,1},{1,0},{2,3},{3,2},{4,5},{5,4},{6,7},{7,6},{8,9},{9,8},{10,11... | collective-permute-start | bytes 61448 | tf_op jit(solution)/shard_map/ppermute | solution.py:250
  61.3 3.3 %collective-permute-start.8 = (f32[40,128]{1,0:T(8,128)S(1)}, f32[40,128]{1,0:T(8,128)S(1)}, u32[]{:S(2)}, u32[]{:S(2)}) collective-permute-start(f32[40,128]{1,0:T(8,128)S(1)} %get-tuple-element.44.refs_0_), channel_id=1, source_target_pairs={{0,3},{1,2},{2,1},{3,0},{4,7},{5,6},{6,5},{7,4},{8,11},{9,10},{10,... | collective-permute-start | bytes 61448 | tf_op jit(solution)/shard_map/ppermute | solution.py:250
  61.3 3.8 %collective-permute-start.7 = (f32[40,128]{1,0:T(8,128)S(1)}, f32[40,128]{1,0:T(8,128)S(1)}, u32[]{:S(2)}, u32[]{:S(2)}) collective-permute-start(f32[40,128]{1,0:T(8,128)S(1)} %get-tuple-element.44.refs_0_), channel_id=1, source_target_pairs={{0,2},{1,3},{2,0},{3,1},{4,6},{5,7},{6,4},{7,5},{8,10},{9,11},{10,... | collective-permute-start | bytes 61448 | tf_op jit(solution)/shard_map/ppermute | solution.py:250
  62.6 2.5 %collective-permute-start.6 = (f32[40,128]{1,0:T(8,128)S(1)}, f32[40,128]{1,0:T(8,128)S(1)}, u32[]{:S(2)}, u32[]{:S(2)}) collective-permute-start(f32[40,128]{1,0:T(8,128)S(1)} %get-tuple-element.44.refs_0_), channel_id=1, source_target_pairs={{0,1},{1,0},{2,3},{3,2},{4,5},{5,4},{6,7},{7,6},{8,9},{9,8},{10,11... | collective-permute-start | bytes 61448 | tf_op jit(solution)/shard_map/ppermute | solution.py:250
  80.0 3.2 %collective-permute-start.11 = (f32[40,128]{1,0:T(8,128)S(1)}, f32[40,128]{1,0:T(8,128)S(1)}, u32[]{:S(2)}, u32[]{:S(2)}) collective-permute-start(f32[40,128]{1,0:T(8,128)S(1)} %get-tuple-element.52.refs_0_), channel_id=1, source_target_pairs={{0,3},{1,2},{2,1},{3,0},{4,7},{5,6},{6,5},{7,4},{8,11},{9,10},{10,... | collective-permute-start | bytes 61448 | tf_op jit(solution)/shard_map/ppermute | solution.py:250
  80.0 3.9 %collective-permute-start.10 = (f32[40,128]{1,0:T(8,128)S(1)}, f32[40,128]{1,0:T(8,128)S(1)}, u32[]{:S(2)}, u32[]{:S(2)}) collective-permute-start(f32[40,128]{1,0:T(8,128)S(1)} %get-tuple-element.52.refs_0_), channel_id=1, source_target_pairs={{0,2},{1,3},{2,0},{3,1},{4,6},{5,7},{6,4},{7,5},{8,10},{9,11},{10,... | collective-permute-start | bytes 61448 | tf_op jit(solution)/shard_map/ppermute | solution.py:250
  80.8 3.1 %collective-permute-start.9 = (f32[40,128]{1,0:T(8,128)S(1)}, f32[40,128]{1,0:T(8,128)S(1)}, u32[]{:S(2)}, u32[]{:S(2)}) collective-permute-start(f32[40,128]{1,0:T(8,128)S(1)} %get-tuple-element.52.refs_0_), channel_id=1, source_target_pairs={{0,1},{1,0},{2,3},{3,2},{4,5},{5,4},{6,7},{7,6},{8,9},{9,8},{10,11... | collective-permute-start | bytes 61448 | tf_op jit(solution)/shard_map/ppermute | solution.py:250
